TPU v7x, 16 devices: a 4x2x1 block of a 4x4x8 slice. The times are simulated.
16 devices in a mesh: dp: 2 (over y, z), cp: 8 (over x, core).
Axes of the slice: x: 4, y: 2, z: 1, core: 2. Of those that a mesh axis runs over, the one named last changes fastest.
The devices are a block of a 4x4x8 slice.
Arguments:
- vis_feat: bfloat16 [16, 4096, 1152], P(('dp', 'cp')), parts along dimension 0
- text_emb: bfloat16 [8192, 2304], P(('dp', 'cp')), parts along dimension 0
- img_pos: int32 [16], P('dp'), parts along dimension 0
- grad_y: bfloat16 [8192, 2304], P(('dp', 'cp')), parts along dimension 0
- pn_gain: bfloat16 [1152], replicated
- w_proj: bfloat16 [1152, 2304], replicated
- pre_gain: bfloat16 [2304], replicated
- w_query: bfloat16 [2304, 2048], replicated
- w_key: bfloat16 [2304, 1024], replicated
- w_value: bfloat16 [2304, 1024], replicated
- q_gain: bfloat16 [256], replicated
- k_gain: bfloat16 [256], replicated
- w_out: bfloat16 [2048, 2304], replicated
- post_gain: bfloat16 [2304], replicated
Outputs:
- output 1: bfloat16 [8192, 2304], P(('dp', 'cp')), parts along dimension 0
- output 2: bfloat16 [8192, 2304], P(('dp', 'cp')), parts along dimension 0
- output 3: bfloat16 [16, 4096, 1152], P(('dp', 'cp')), parts along dimension 0
- output 4: bfloat16 [2304], P('dp'), parts along dimension 0
- output 5: bfloat16 [2304, 2304], P('dp'), parts along dimension 0
- output 6: bfloat16 [4608], P('dp'), parts along dimension 0
- output 7: bfloat16 [4608, 2048], P('dp'), parts along dimension 0
- output 8: bfloat16 [4608, 1024], P('dp'), parts along dimension 0
- output 9: bfloat16 [4608, 1024], P('dp'), parts along dimension 0
- output 10: bfloat16 [512], P('dp'), parts along dimension 0
- output 11: bfloat16 [512], P('dp'), parts along dimension 0
- output 12: bfloat16 [4096, 2304], P('dp'), parts along dimension 0
- output 13: bfloat16 [4608], P('dp'), parts along dimension 0
There are 2 independent parts. A program takes and returns all parts, laid end to end along the dimension named above; an argument that names none is the same for every part.
All inputs are finite; a program needn't handle non-finite values.
Results may differ from a plain program's by a relative error of at most 0.02.
Values are sent between devices in bfloat16 or wider.
A program may use at most 768 MiB of HBM per device.

v0:
```python
import functools
import jax
import jax.numpy as jnp
from jax import lax
from jax.sharding import PartitionSpec as P

GRID = 64
POOL = 4
EPS = 1e-6
ROPE_BASE = 1000000.0
ROPE_SCALE = 8.0
NEG_BIG = -1e30


def rms_scale(values, gain_vec):
    wide_vals = values.astype(jnp.float32)
    mean_sq = jnp.mean(wide_vals * wide_vals, axis=-1, keepdims=True)
    return wide_vals * lax.rsqrt(mean_sq + EPS) * (1.0 + gain_vec)


def gain_norm(values, gain_vec):
    return rms_scale(values, gain_vec).astype(jnp.bfloat16)


def rope_tables(positions, head_dim):
    inv_freq = ROPE_BASE ** (-jnp.arange(0, head_dim, 2).astype(jnp.float32) / head_dim)
    rot_angle = (positions.astype(jnp.float32) / ROPE_SCALE)[:, None] * inv_freq[None, :]
    rot_angle = jnp.concatenate([rot_angle, rot_angle], axis=-1)
    return jnp.cos(rot_angle)[:, None, :], jnp.sin(rot_angle)[:, None, :]


def apply_rope(values, cos_t, sin_t):
    half_dim = values.shape[-1] // 2
    rotated = jnp.concatenate([-values[..., half_dim:], values[..., :half_dim]], axis=-1)
    return values * cos_t + rotated * sin_t


def qk_rotate(q_raw, k_raw, q_gain, k_gain, cos_t, sin_t):
    q_heads = apply_rope(rms_scale(q_raw, q_gain), cos_t, sin_t).astype(jnp.bfloat16)
    k_heads = apply_rope(rms_scale(k_raw, k_gain), cos_t, sin_t).astype(jnp.bfloat16)
    return q_heads, k_heads


def post_residual(merged, proj_out, gain_vec):
    return (merged.astype(jnp.float32) + rms_scale(proj_out, gain_vec)).astype(jnp.bfloat16)


def pool_patches(vis_loc):
    img_count = vis_loc.shape[0]
    dim_v = vis_loc.shape[2]
    side_len = GRID // POOL
    patch_grid = vis_loc.reshape(img_count, side_len, POOL, side_len, POOL, dim_v)
    pooled = jnp.sum(patch_grid, axis=(2, 4), dtype=jnp.float32) / (POOL * POOL)
    return pooled.astype(jnp.bfloat16).reshape(img_count * side_len * side_len, dim_v)


def unpool_grad(d_pooled, img_count):
    side_len = GRID // POOL
    dim_v = d_pooled.shape[-1]
    spread = (d_pooled.astype(jnp.float32) / (POOL * POOL)).reshape(img_count, side_len, 1, side_len, 1, dim_v)
    spread = jnp.broadcast_to(spread, (img_count, side_len, POOL, side_len, POOL, dim_v))
    return spread.astype(jnp.bfloat16).reshape(img_count, GRID * GRID, dim_v)


def merge_layout(img_pos, dev_rank, seq_loc, block_len):
    q_pos = dev_rank * seq_loc + jnp.arange(seq_loc)
    offset = q_pos[:, None] - img_pos[None, :]
    in_blk = (offset >= 0) & (offset < block_len)
    is_img = jnp.any(in_blk, axis=1)
    flat_row = jnp.sum(jnp.where(in_blk, jnp.arange(img_pos.shape[0])[None, :] * block_len + offset, 0), axis=1)
    blk_start = jnp.where(is_img, q_pos - jnp.sum(jnp.where(in_blk, offset, 0), axis=1), -block_len)
    return q_pos, is_img, flat_row, blk_start


def attn_forward(q_heads, k_all, v_all, visible):
    seq_loc = q_heads.shape[0]
    head_dim = q_heads.shape[-1]
    q_grp = q_heads.reshape(seq_loc, k_all.shape[1], -1, head_dim)
    scores = jnp.einsum('qkgd,skd->kgqs', q_grp, k_all, preferred_element_type=jnp.float32) * head_dim ** -0.5
    probs_hi = jax.nn.softmax(jnp.where(visible, scores, NEG_BIG), axis=-1)
    probs_lo = probs_hi.astype(jnp.bfloat16)
    attn_out = jnp.einsum('kgqs,skd->qkgd', probs_lo, v_all, preferred_element_type=jnp.float32)
    return attn_out.astype(jnp.bfloat16).reshape(seq_loc, -1), probs_hi, probs_lo


def attn_backward(d_attn, q_heads, k_all, v_all, probs_hi, probs_lo):
    seq_loc = q_heads.shape[0]
    head_dim = q_heads.shape[-1]
    q_grp = q_heads.reshape(seq_loc, k_all.shape[1], -1, head_dim)
    d_grp = d_attn.reshape(q_grp.shape)
    d_probs = jnp.einsum('qkgd,skd->kgqs', d_grp, v_all, preferred_element_type=jnp.float32)
    d_v_part = jnp.einsum('kgqs,qkgd->skd', probs_lo, d_grp, preferred_element_type=jnp.float32)
    d_scores = probs_hi * (d_probs - jnp.sum(d_probs * probs_hi, axis=-1, keepdims=True)) * head_dim ** -0.5
    d_scores = d_scores.astype(jnp.bfloat16)
    d_q = jnp.einsum('kgqs,skd->qkgd', d_scores, k_all, preferred_element_type=jnp.float32).astype(jnp.bfloat16).reshape(q_heads.shape)
    d_k_part = jnp.einsum('kgqs,qkgd->skd', d_scores, q_grp, preferred_element_type=jnp.float32)
    return d_q, d_k_part, d_v_part


def solution(mesh):
    group_size = mesh.shape['cp']
    seq_spec = P(('dp', 'cp'))
    part_spec = P('dp')
    rep_spec = P()

    def device_body(vis_loc, text_loc, img_pos, grad_y, pn_gain, w_proj, pre_gain, w_query, w_key, w_value, q_gain, k_gain, w_out, post_gain):
        dev_rank = lax.axis_index('cp')
        seq_loc = text_loc.shape[0]
        img_loc = vis_loc.shape[0]
        head_dim = q_gain.shape[0]
        block_len = (GRID // POOL) ** 2
        pooled = pool_patches(vis_loc)
        normed, norm_pull = jax.vjp(gain_norm, pooled, pn_gain.astype(jnp.float32))
        soft_loc = jnp.dot(normed, w_proj, preferred_element_type=jnp.float32).astype(jnp.bfloat16)
        soft_all = lax.all_gather(soft_loc, 'cp', tiled=True)
        q_pos, is_img, flat_row, blk_start = merge_layout(img_pos, dev_rank, seq_loc, block_len)
        img_mask = is_img[:, None]
        merged = jnp.where(img_mask, jnp.take(soft_all, flat_row, axis=0), text_loc)
        hidden, pre_pull = jax.vjp(gain_norm, merged, pre_gain.astype(jnp.float32))
        q_raw = jnp.dot(hidden, w_query, preferred_element_type=jnp.float32).astype(jnp.bfloat16).reshape(seq_loc, -1, head_dim)
        k_raw = jnp.dot(hidden, w_key, preferred_element_type=jnp.float32).astype(jnp.bfloat16).reshape(seq_loc, -1, head_dim)
        v_loc = jnp.dot(hidden, w_value, preferred_element_type=jnp.float32).astype(jnp.bfloat16).reshape(seq_loc, -1, head_dim)
        cos_t, sin_t = rope_tables(q_pos, head_dim)
        rotate_fn = functools.partial(qk_rotate, cos_t=cos_t, sin_t=sin_t)
        (q_heads, k_loc), qk_pull = jax.vjp(rotate_fn, q_raw, k_raw, q_gain.astype(jnp.float32), k_gain.astype(jnp.float32))
        k_all = lax.all_gather(k_loc, 'cp', tiled=True)
        v_all = lax.all_gather(v_loc, 'cp', tiled=True)
        key_pos = jnp.arange(seq_loc * group_size)
        visible = (key_pos[None, :] <= q_pos[:, None]) | ((key_pos[None, :] >= blk_start[:, None]) & (key_pos[None, :] < blk_start[:, None] + block_len))
        attn_out, probs_hi, probs_lo = attn_forward(q_heads, k_all, v_all, visible)
        proj_out = jnp.dot(attn_out, w_out, preferred_element_type=jnp.float32).astype(jnp.bfloat16)
        y_loc, post_pull = jax.vjp(post_residual, merged, proj_out, post_gain.astype(jnp.float32))
        d_resid, d_proj, g_post = post_pull(grad_y)
        g_out = jnp.einsum('sh,sd->hd', attn_out, d_proj, preferred_element_type=jnp.float32)
        d_attn = jnp.einsum('sd,hd->sh', d_proj, w_out, preferred_element_type=jnp.float32).astype(jnp.bfloat16)
        d_q, d_k_part, d_v_part = attn_backward(d_attn, q_heads, k_all, v_all, probs_hi, probs_lo)
        d_k_loc = lax.psum_scatter(d_k_part, 'cp', scatter_dimension=0, tiled=True).astype(jnp.bfloat16)
        d_v_loc = lax.psum_scatter(d_v_part, 'cp', scatter_dimension=0, tiled=True).astype(jnp.bfloat16)
        d_q_raw, d_k_raw, g_q_gain, g_k_gain = qk_pull((d_q, d_k_loc))
        d_q_flat = d_q_raw.reshape(seq_loc, -1)
        d_k_flat = d_k_raw.reshape(seq_loc, -1)
        d_v_flat = d_v_loc.reshape(seq_loc, -1)
        d_hidden = jnp.einsum('sh,dh->sd', d_q_flat, w_query, preferred_element_type=jnp.float32)
        d_hidden = d_hidden + jnp.einsum('sh,dh->sd', d_k_flat, w_key, preferred_element_type=jnp.float32)
        d_hidden = (d_hidden + jnp.einsum('sh,dh->sd', d_v_flat, w_value, preferred_element_type=jnp.float32)).astype(jnp.bfloat16)
        g_query = jnp.einsum('sd,sh->dh', hidden, d_q_flat, preferred_element_type=jnp.float32)
        g_key = jnp.einsum('sd,sh->dh', hidden, d_k_flat, preferred_element_type=jnp.float32)
        g_value = jnp.einsum('sd,sh->dh', hidden, d_v_flat, preferred_element_type=jnp.float32)
        d_merged_attn, g_pre = pre_pull(d_hidden)
        d_merged = (d_resid.astype(jnp.float32) + d_merged_attn.astype(jnp.float32)).astype(jnp.bfloat16)
        grad_text = jnp.where(img_mask, 0.0, d_merged).astype(jnp.bfloat16)
        d_soft_all = jnp.zeros_like(soft_all).at[flat_row].add(jnp.where(img_mask, d_merged, 0.0).astype(jnp.bfloat16))
        d_soft_loc = lax.psum_scatter(d_soft_all, 'cp', scatter_dimension=0, tiled=True)
        g_proj = jnp.einsum('nc,nd->cd', normed, d_soft_loc, preferred_element_type=jnp.float32)
        d_normed = jnp.einsum('nd,cd->nc', d_soft_loc, w_proj, preferred_element_type=jnp.float32).astype(jnp.bfloat16)
        d_pooled, g_pn = norm_pull(d_normed)
        grad_vis = unpool_grad(d_pooled, img_loc)
        weight_grads = lax.psum((g_pn, g_proj, g_pre, g_query, g_key, g_value, g_q_gain, g_k_gain, g_out, g_post), 'cp')
        return (y_loc, grad_text, grad_vis) + tuple(grad_part.astype(jnp.bfloat16) for grad_part in weight_grads)

    in_specs = (seq_spec, seq_spec, part_spec, seq_spec) + (rep_spec,) * 10
    out_specs = (seq_spec, seq_spec, seq_spec) + (part_spec,) * 10
    return jax.shard_map(device_body, mesh=mesh, in_specs=in_specs, out_specs=out_specs, check_vma=False)
```

profile of v0, /device:TPU:113, one launch (start us, length us, event | category | flops | bytes accessed | tf_op | source)
XLA Modules:
  0.0 1399.9 jit_solution(10280695860744749380)
XLA Ops:
  7.3 17.8 %reshape.340 = f32[16,4,16,4,1152]{4,3,2,1,0:T(4,128)} reshape(bf16[1,4096,1152]{2,1,0:T(8,128)(2,1)} %param.14) | data formatting | bytes 28311552 | tf_op jit(solution)/shard_map/convert_element_type | solution.py:53
  25.1 11.6 reduce_sum.181
  38.1 5.3 convolution_convert_fusion.1
  46.7 50.1 %all-gather.4.cloned.1.call-done = bf16[2048,2304]{1,0:T(8,128)(2,1)} async-done(((bf16[256,2304]{1,0:T(8,128)(2,1)}), bf16[2048,2304]{1,0:T(8,128)(2,1)}) %all-gather.4.cloned.1.call-update) | async-done | bytes 9437200 | tf_op jit(solution)/shard_map/all_gather | solution.py:115
  96.8 9.8 gather_fusion
  121.9 6.7 convolution_convert_fusion.6
  136.7 10.4 fusion.47
  147.2 5.3 copy.215
  176.2 27.6 %fusion.19 = f32[4,4096,512,2]{2,1,3,0:T(8,128)} fusion(bf16[512,4,2,256]{0,3,2,1:T(8,128)(2,1)S(1)} %fusion.46, bf16[4096,4,256]{2,0,1:T(8,128)(2,1)} %all-gather.8.cloned.1.call-done), kind=kOutput, calls=%fused_computation.30 | convolution fusion | flops 8589934592 | bytes 77594624 | tf_op jit(solution)/shard_map/qkgd,skd->kgqs/dot_general | solution.py:79
  203.8 66.6 %fusion.107 = (f32[4,2,512]{2,1,0:T(2,128)S(1)}, f32[4,2,512,4096]{2,3,1,0:T(8,128)}) fusion(f32[4,4096,512,2]{2,1,3,0:T(8,128)} %fusion.19, pred[512,4096]{0,1:T(8,128)(4,1)} %fusion.24), kind=kOutput, calls=%fused_computation.187 | output fusion | flops 100667392 | bytes 136331264 | tf_op jit(solution)/shard_map/sub | solution.py:80
  270.4 25.3 %fusion.60 = bf16[4,256,2,512]{3,1,2,0:T(8,128)(2,1)S(1)} fusion(bf16[4096,4,256]{0,2,1:T(8,128)(2,1)} %all-gather.6.cloned.1.call-done, f32[4,2,512,4096]{2,3,1,0:T(8,128)} %get-tuple-element.57, f32[4,2,512]{2,1,0:T(2,128)S(1)} %get-tuple-element.56), kind=kOutput, calls=%fused_computation.112 | convolution fusion | flops 8624537600 | bytes 77611008 | tf_op jit(solution)/shard_map/kgqs,skd->qkgd/dot_general | solution.py:82
  295.8 9.9 fusion.36
  311.3 6.6 convolution_convert_fusion.2
  320.8 26.8 %fusion.21 = f32[4,4096,512,2]{2,1,3,0:T(8,128)} fusion(bf16[512,4,2,256]{0,3,2,1:T(8,128)(2,1)S(1)} %bitcast.160, bf16[4096,4,256]{0,2,1:T(8,128)(2,1)} %all-gather.6.cloned.1.call-done), kind=kOutput, calls=%fused_computation.32 | convolution fusion | flops 8589934592 | bytes 77594624 | tf_op jit(solution)/shard_map/qkgd,skd->kgqs/dot_general | solution.py:91
  347.6 87.7 %convolution_bitcast_fusion = f32[4096,4,256]{2,0,1:T(8,128)} fusion(bf16[512,4,2,256]{0,3,2,1:T(8,128)(2,1)} %copy-done.17, f32[4,4096,512,2]{2,1,3,0:T(8,128)} %fusion.21, f32[4,2,512,4096]{2,3,1,0:T(8,128)} %get-tuple-element.57, f32[4,2,512]{2,1,0:T(2,128)S(1)} %get-tuple-element.56), kind=kOutput, calls=%fused_computation.27 | convolution fusion | flops 8707383296 | bytes 153108480 | tf_op jit(solution)/shard_map/kgqs,qkgd->skd/dot_general | solution.py:96
  435.5 29.2 %fusion.14 = f32[4096,4,256]{0,2,1:T(8,128)} fusion(bf16[512,4,2,256]{0,3,2,1:T(8,128)(2,1)S(1)} %bitcast.161, f32[4,2,512,4096]{2,3,1,0:T(8,128)} %get-tuple-element.57, f32[4,2,512]{2,1,0:T(2,128)S(1)} %get-tuple-element.56), kind=kOutput, calls=%fused_computation.26 | convolution fusion | flops 8623489024 | bytes 85999616 | tf_op jit(solution)/shard_map/kgqs,qkgd->skd/dot_general | solution.py:92
  464.8 85.9 %convert_convert_fusion = f32[4,256,2,512]{3,1,2,0:T(8,128)} fusion(f32[4,4096,512,2]{2,1,3,0:T(8,128)} %fusion.21, bf16[4096,4,256]{2,0,1:T(8,128)(2,1)} %all-gather.8.cloned.1.call-done, f32[4,2,512,4096]{2,3,1,0:T(8,128)} %get-tuple-element.57, f32[4,2,512]{2,1,0:T(2,128)S(1)} %get-tuple-element.56), kind=kOutput, calls=%fused_computation.109 | convolution fusion | flops 8709480448 | bytes 146817024 | tf_op jit(solution)/shard_map/kgqs,skd->qkgd/dot_general | solution.py:95
  550.8 5.5 copy.192
  579.3 5.4 fusion.108
  584.8 11.0 convolution_add_fusion
  595.7 16.6 %reduce-scatter.6.cloned.1.call-done = f32[512,4,256]{0,2,1:T(8,128)} async-done(((f32[4096,4,256]{0,2,1:T(8,128)}), f32[512,4,256]{0,2,1:T(8,128)}) %reduce-scatter.6.cloned.1.call-update) | async-done | bytes 2097168 | tf_op jit(solution)/shard_map/reduce_scatter | solution.py:138
  614.2 7.5 fusion.31
  625.2 14.6 %scatter_custom_fusion = bf16[2048,2304]{1,0:T(8,128)(2,1)} fusion(s32[512]{0:T(512)} %bitcast.176, bf16[]{:T(256)} %constant.44.clone.1, bf16[512,2304]{1,0:T(8,128)(2,1)} %get-tuple-element.36, pred[512]{0:T(512)(128)(4,1)S(1)} %copy-done.53), kind=kCustom, calls=%fused_computation.69 | custom fusion | flops 2359296 | bytes 11798016 | tf_op jit(solution)/shard_map/scatter-add | solution.py:152
  639.9 11.2 fusion.98
  651.2 9.4 fusion.91
  660.6 5.3 fusion.96
  666.0 5.4 fusion.94
  671.4 21.7 %reduce-scatter.8.cloned.1.call-done = bf16[256,2304]{1,0:T(8,128)(2,1)} async-done(((bf16[2048,2304]{1,0:T(8,128)(2,1)}), bf16[256,2304]{1,0:T(8,128)(2,1)}) %reduce-scatter.8.cloned.1.call-update) | async-done | bytes 1179664 | tf_op jit(solution)/shard_map/reduce_scatter | solution.py:153
  698.2 5.6 broadcast_in_dim.117
  703.8 15.8 %broadcast_in_dim.118 = bf16[1,4096,1152]{2,1,0:T(8,128)(2,1)} reshape(bf16[16,4,16,4,1152]{4,3,2,1,0:T(4,128)(2,1)} %broadcast_in_dim.117) | data formatting | bytes 18874368 | tf_op jit(solution)/shard_map/broadcast_in_dim | solution.py:61
  719.7 5.6 fusion.109
  725.3 667.3 %all-reduce.6 = (bf16[1152]{0:T(1024)(128)(2,1)}, bf16[1152,2304]{1,0:T(8,128)(2,1)}, bf16[2304]{0:T(1024)(128)(2,1)}, bf16[2304,2048]{1,0:T(8,128)(2,1)}, bf16[...) all-reduce(f32[1152]{0:T(1024)S(1)} %get-tuple-element.21, ...), channel_id=1, replica_groups=mesh['dp'=2,'cp'=8] {'cp'}, use_global_device_ids=true, to_apply=%region_22.23 | all-reduce | flops 16816256 | bytes 100897536 | tf_op jit(solution)/shard_map/psum | solution.py:158
  (234 shorter events, 93.4 us)
Async XLA Ops:
  7.2 89.6 %all-gather.4.cloned.1.call-start = ((), (), s32[]{:S(2)}) async-start(), calls=%async_computation.3 | async-start | bytes 10616832 | tf_op jit(solution)/shard_map/all_gather | solution.py:115
  25.1 11.8 copy-start.65
  43.5 132.7 %all-gather.8.cloned.1.call-start = ((), (), s32[]{:S(2)}) async-start(), calls=%async_computation.5 | async-start | bytes 9437184 | tf_op jit(solution)/shard_map/all_gather | solution.py:126
  44.6 88.2 %copy-start.52 = (pred[512]{0:T(512)(128)(4,1)}, pred[512]{0:T(512)(128)(4,1)S(1)}, u32[]{:S(2)}) copy-start(pred[512]{0:T(512)(128)(4,1)S(1)} %fusion.81) | copy-start | bytes 1540
  46.6 85.0 %copy-start.11 = (f32[512,256]{1,0:T(8,128)}, f32[512,256]{1,0:T(8,128)S(1)}, u32[]{:S(2)}) copy-start(f32[512,256]{1,0:T(8,128)S(1)} %get-tuple-element.55) | copy-start | bytes 1572868
  46.6 86.0 %copy-start.9 = (f32[512,256]{1,0:T(8,128)}, f32[512,256]{1,0:T(8,128)S(1)}, u32[]{:S(2)}) copy-start(f32[512,256]{1,0:T(8,128)S(1)} %get-tuple-element.54) | copy-start | bytes 1572868
  46.7 73.6 %copy-start.50 = (f32[256]{0:T(256)}, f32[256]{0:T(256)S(1)}, u32[]{:S(2)}) copy-start(f32[256]{0:T(256)S(1)} %convert_add_fusion.6) | copy-start | bytes 3076
  46.7 90.0 %copy-start.42 = (f32[2304]{0:T(1024)}, f32[2304]{0:T(1024)S(1)}, u32[]{:S(2)}) copy-start(f32[2304]{0:T(1024)S(1)} %convert_add_fusion.3) | copy-start | bytes 27652
  109.4 27.4 %copy-start.58 = (f32[512]{0:T(512)}, f32[512]{0:T(512)S(1)}, u32[]{:S(2)}) copy-start(f32[512]{0:T(512)S(1)} %fusion.83) | copy-start | bytes 6148
  121.9 148.5 %all-gather.6.cloned.1.call-start = ((), (), s32[]{:S(2)}) async-start(), calls=%async_computation.4 | async-start | bytes 9437184 | tf_op jit(solution)/shard_map/all_gather | solution.py:127
  131.1 442.9 %reduce-scatter.4.cloned.1.call-start = ((), (), s32[]{:S(2)}) async-start(), calls=%async_computation.6 | async-start | bytes 18874368 | tf_op jit(solution)/shard_map/reduce_scatter | solution.py:137
  132.8 38.5 %copy-start.48 = (f32[256]{0:T(256)}, f32[256]{0:T(256)S(1)}, u32[]{:S(2)}) copy-start(f32[256]{0:T(256)S(1)} %convert_add_fusion.5) | copy-start | bytes 3076
  176.2 27.6 %copy-start.17 = (bf16[512,4,2,256]{0,3,2,1:T(8,128)(2,1)}, bf16[512,4,2,256]{0,3,2,1:T(8,128)(2,1)S(1)}, u32[]{:S(2)}) copy-start(bf16[512,4,2,256]{0,3,2,1:T(8,128)(2,1)S(1)} %fusion.46) | copy-start | bytes 6291460
  295.8 10.0 copy-start.7
  295.8 10.0 copy-start.13
  435.4 177.0 %reduce-scatter.6.cloned.1.call-start = ((), (), s32[]{:S(2)}) async-start(), calls=%async_computation.7 | async-start | bytes 18874368 | tf_op jit(solution)/shard_map/reduce_scatter | solution.py:138
  464.8 228.3 %reduce-scatter.8.cloned.1.call-start = ((), (), s32[]{:S(2)}) async-start(), calls=%async_computation.8 | async-start | bytes 10616832 | tf_op jit(solution)/shard_map/reduce_scatter | solution.py:153
  584.8 29.3 %copy-start.8 = (bf16[512,2304]{1,0:T(8,128)(2,1)S(1)}, bf16[512,2304]{1,0:T(8,128)(2,1)}, u32[]{:S(2)}) copy-start(bf16[512,2304]{1,0:T(8,128)(2,1)} %copy-done.5) | copy-start | bytes 7077892
  584.8 29.3 %copy-start.43 = (f32[2304]{0:T(1024)S(1)}, f32[2304]{0:T(1024)}, u32[]{:S(2)}) copy-start(f32[2304]{0:T(1024)} %copy-done.42) | copy-start | bytes 27652
  584.8 29.3 %copy-start.59 = (f32[512]{0:T(512)S(1)}, f32[512]{0:T(512)}, u32[]{:S(2)}) copy-start(f32[512]{0:T(512)} %copy-done.58) | copy-start | bytes 6148
  639.9 11.3 copy-start.15
  639.9 11.3 copy-start.25
  639.9 11.3 copy-start.45
  639.9 11.3 copy-start.61
  639.9 11.3 copy-start.68
  639.9 11.3 copy-start.73
  666.0 27.1 %copy-start.19 = (bf16[16,16,1152]{2,1,0:T(8,128)(2,1)S(1)}, bf16[16,16,1152]{2,1,0:T(8,128)(2,1)}, u32[]{:S(2)}) copy-start(bf16[16,16,1152]{2,1,0:T(8,128)(2,1)} %copy-done.18) | copy-start | bytes 1769476
  666.0 27.1 %copy-start.38 = (f32[1152]{0:T(1024)S(1)}, f32[1152]{0:T(1024)}, u32[]{:S(2)}) copy-start(f32[1152]{0:T(1024)} %copy-done.37) | copy-start | bytes 13828
  666.0 27.1 %copy-start.57 = (f32[256]{0:T(256)S(1)}, f32[256]{0:T(256)}, u32[]{:S(2)}) copy-start(f32[256]{0:T(256)} %copy-done.56) | copy-start | bytes 3076
  671.4 26.4 %copy-start.55 = (f32[256]{0:T(256)S(1)}, f32[256]{0:T(256)}, u32[]{:S(2)}) copy-start(f32[256]{0:T(256)} %copy-done.54) | copy-start | bytes 3076
  703.8 15.9 %copy-start.23 = (bf16[256,1152]{1,0:T(8,128)(2,1)S(1)}, bf16[256,1152]{1,0:T(8,128)(2,1)}, u32[]{:S(2)}) copy-start(bf16[256,1152]{1,0:T(8,128)(2,1)} %copy-done.22) | copy-start | bytes 1769476
  703.8 15.9 %copy-start.28 = (bf16[256,2304]{1,0:T(8,128)(2,1)S(1)}, bf16[256,2304]{1,0:T(8,128)(2,1)}, u32[]{:S(2)}) copy-start(bf16[256,2304]{1,0:T(8,128)(2,1)} %reduce-scatter.8.cloned.1.call-done) | copy-start | bytes 3538948
  (48 other events, 224.3 us)
Sparse Core Ops, SparseCore 0:
  43.6 53.1 all-gather.3
  122.0 45.6 all-gather.7
  169.9 45.6 all-gather.5
  435.5 87.1 reduce-scatter.3
  524.9 87.3 reduce-scatter.5
  640.0 53.0 reduce-scatter.7
where the time goes:
time: 1410 us; the launch traced here: 1400 us
  blocking collectives  667 us (47%)
  matrix products  392 us (28%)
  other arithmetic  143 us (10%)
  local copies, waits for them, and re-layouts  92.9 us (7%)
  waiting for transfers between devices  88.8 us (6%)
  between operations  15.7 us (1%)
    psum x1, blocking collectives, device_body(): lax.psum((g_pn, g_proj, g_pre, g_query, g_key, g_value, g_q_gain, g_k_gai...  667 us
    dot_general x1, matrix products, attn_backward(): jnp.einsum('kgqs,qkgd->skd', d_scores, q_grp, preferred_element_type=jnp....  87.7 us
    dot_general x1, matrix products, attn_backward(): jnp.einsum('kgqs,skd->qkgd', d_scores, k_all, preferred_element_type=jnp....  85.9 us
    sub x1, other arithmetic, attn_forward(): probs_hi = jax.nn.softmax(jnp.where(visible, scores, NEG_BIG), axis=-1)  66.6 us
    all_gather x1, waiting for transfers between devices, device_body(): soft_all = lax.all_gather(soft_loc, 'cp', tiled=True)  50.1 us
    dot_general x1, matrix products, attn_backward(): jnp.einsum('kgqs,qkgd->skd', probs_lo, d_grp, preferred_element_type=jnp....  29.2 us
  transfers between devices with their start and end apart: 6, of which 3 were waited for; matrix products, arithmetic and copies ran while one was open for 24% of the time, Pallas kernels for 0%

commit v1 on v0

v1 whole, which is shorter than its diff:
```python
import functools
import jax
import jax.numpy as jnp
from jax import lax
from jax.experimental import pallas as pl
from jax.experimental.pallas import tpu as pltpu
from jax.sharding import PartitionSpec as P

GRID = 64
POOL = 4
EPS = 1e-6
ROPE_BASE = 1000000.0
ROPE_SCALE = 8.0
NEG_BIG = -1e30
BF = jnp.bfloat16
F32 = jnp.float32


def rms_scale(values, gain_vec):
    wide_vals = values.astype(F32)
    mean_sq = jnp.mean(wide_vals * wide_vals, axis=-1, keepdims=True)
    return wide_vals * lax.rsqrt(mean_sq + EPS) * (1.0 + gain_vec)


def gain_norm(values, gain_vec):
    return rms_scale(values, gain_vec).astype(BF)


def rope_tables(positions, head_dim):
    inv_freq = ROPE_BASE ** (-jnp.arange(0, head_dim, 2).astype(F32) / head_dim)
    rot_angle = (positions.astype(F32) / ROPE_SCALE)[:, None] * inv_freq[None, :]
    rot_angle = jnp.concatenate([rot_angle, rot_angle], axis=-1)
    return jnp.cos(rot_angle), jnp.sin(rot_angle)


def apply_rope(values, cos_t, sin_t):
    half_dim = values.shape[-1] // 2
    rotated = jnp.concatenate([-values[..., half_dim:], values[..., :half_dim]], axis=-1)
    return values * cos_t + rotated * sin_t


def head_rotate(raw, gain, cos_t, sin_t):
    return apply_rope(rms_scale(raw, gain), cos_t, sin_t).astype(BF)


def post_residual(merged, proj_out, gain_vec):
    return (merged.astype(F32) + rms_scale(proj_out, gain_vec)).astype(BF)


def mm(a, b, dims=((1,), (0,))):
    return lax.dot_general(a, b, (dims, ((), ())), preferred_element_type=F32)


def attn_fwd_body(lmax_ref, lim_ref, q_ref, k_ref, vt_ref, o_ref, of_ref, lse_ref, acc_ref, m_ref, l_ref, *, bq, bo):
    qi = pl.program_id(0)
    q0 = qi * bq
    acc_ref[...] = jnp.zeros_like(acc_ref)
    m_ref[...] = jnp.full_like(m_ref, NEG_BIG)
    l_ref[...] = jnp.zeros_like(l_ref)
    q = q_ref[...]

    def tile(k0, bk, masked):
        s = mm(k_ref[pl.ds(k0, bk), :], q, ((1,), (1,)))
        if masked:
            kpos = k0 + lax.broadcasted_iota(jnp.int32, s.shape, 0)
            s = jnp.where(kpos <= lim_ref[0], s, NEG_BIG)
        m_old = m_ref[...]
        m_new = jnp.maximum(m_old, jnp.max(s, axis=0, keepdims=True))
        p = jnp.exp(s - m_new)
        alpha = jnp.exp(m_old - m_new)
        m_ref[...] = m_new
        l_ref[...] = l_ref[...] * alpha + jnp.sum(p, axis=0, keepdims=True)
        acc_ref[...] = acc_ref[...] * alpha + mm(vt_ref[:, pl.ds(k0, bk)], p.astype(BF))

    def step(kb, carry):
        tile(pl.multiple_of(kb * bq, bq), bq, False)
        return carry

    lax.fori_loop(0, qi, step, 0)
    tile(pl.multiple_of(q0, bq), bq, True)

    @pl.when(lmax_ref[qi] >= q0 + bq)
    def _():
        tile(pl.multiple_of(q0 + bq, bq), bo, True)

    l = l_ref[...]
    o = jnp.transpose(acc_ref[...] / l)
    of_ref[...] = o
    o_ref[...] = o.astype(BF)
    lse_ref[0] = m_ref[...] + jnp.log(l)


def attn_fwd(q, k, vt, lim, lmax, bq, bo):
    seq, hd = q.shape
    nq = seq // bq
    body = functools.partial(attn_fwd_body, bq=bq, bo=bo)
    row = pl.BlockSpec((1, 1, bq), lambda i, s: (i, 0, 0))
    tile = pl.BlockSpec((bq, hd), lambda i, s: (i, 0))
    return pl.pallas_call(
        body,
        out_shape=(jax.ShapeDtypeStruct((seq, hd), BF), jax.ShapeDtypeStruct((seq, hd), F32), jax.ShapeDtypeStruct((nq, 1, bq), F32)),
        grid_spec=pltpu.PrefetchScalarGridSpec(
            num_scalar_prefetch=1,
            grid=(nq,),
            in_specs=[row, tile, pl.BlockSpec((seq, hd), lambda i, s: (0, 0)), pl.BlockSpec((hd, seq), lambda i, s: (0, 0))],
            out_specs=(tile, tile, row),
            scratch_shapes=[pltpu.VMEM((hd, bq), F32), pltpu.VMEM((1, bq), F32), pltpu.VMEM((1, bq), F32)],
        ),
        compiler_params=pltpu.CompilerParams(dimension_semantics=('arbitrary',), vmem_limit_bytes=48 * 1024 * 1024),
        cost_estimate=pl.CostEstimate(flops=2 * seq * seq * hd, bytes_accessed=seq * hd * 14, transcendentals=seq * seq // 2),
        name='attn_fwd',
    )(lmax, lim, q, k, vt)


def attn_bwd_body(lmax_ref, lim_ref, lse_ref, dl_ref, q_ref, do_ref, k_ref, kt_ref, v_ref, dq_ref, dk_ref, dv_ref, acc_ref, *, bq, bo, scale):
    qi = pl.program_id(0)
    q0 = qi * bq

    @pl.when(qi == 0)
    def _():
        dk_ref[...] = jnp.zeros_like(dk_ref)
        dv_ref[...] = jnp.zeros_like(dv_ref)

    acc_ref[...] = jnp.zeros_like(acc_ref)
    q = q_ref[...]
    do = do_ref[...]
    lse = lse_ref[0]
    delta = dl_ref[0]

    def tile(k0, bk, masked):
        ks = pl.ds(k0, bk)
        s = mm(k_ref[ks, :], q, ((1,), (1,)))
        if masked:
            kpos = k0 + lax.broadcasted_iota(jnp.int32, s.shape, 0)
            s = jnp.where(kpos <= lim_ref[0], s, NEG_BIG)
        p = jnp.exp(s - lse)
        dp = mm(v_ref[ks, :], do, ((1,), (1,)))
        dv_ref[ks, :] += mm(p.astype(BF), do)
        ds = (p * (dp - delta)).astype(BF)
        dk_ref[ks, :] += mm(ds, q)
        acc_ref[...] += mm(kt_ref[:, ks], ds)

    def step(kb, carry):
        tile(pl.multiple_of(kb * bq, bq), bq, False)
        return carry

    lax.fori_loop(0, qi, step, 0)
    tile(pl.multiple_of(q0, bq), bq, True)

    @pl.when(lmax_ref[qi] >= q0 + bq)
    def _():
        tile(pl.multiple_of(q0 + bq, bq), bo, True)

    dq_ref[...] = (jnp.transpose(acc_ref[...]) * scale).astype(BF)


def attn_bwd(q, k, kt, v, do, lse, delta, lim, lmax, bq, bo, scale):
    seq, hd = q.shape
    nq = seq // bq
    body = functools.partial(attn_bwd_body, bq=bq, bo=bo, scale=scale)
    row = pl.BlockSpec((1, 1, bq), lambda i, s: (i, 0, 0))
    tile = pl.BlockSpec((bq, hd), lambda i, s: (i, 0))
    whole = pl.BlockSpec((seq, hd), lambda i, s: (0, 0))
    return pl.pallas_call(
        body,
        out_shape=(jax.ShapeDtypeStruct((seq, hd), BF), jax.ShapeDtypeStruct((seq, hd), F32), jax.ShapeDtypeStruct((seq, hd), F32)),
        grid_spec=pltpu.PrefetchScalarGridSpec(
            num_scalar_prefetch=1,
            grid=(nq,),
            in_specs=[row, row, row, tile, tile, whole, pl.BlockSpec((hd, seq), lambda i, s: (0, 0)), whole],
            out_specs=(tile, whole, whole),
            scratch_shapes=[pltpu.VMEM((hd, bq), F32)],
        ),
        compiler_params=pltpu.CompilerParams(dimension_semantics=('arbitrary',), vmem_limit_bytes=56 * 1024 * 1024),
        cost_estimate=pl.CostEstimate(flops=5 * seq * seq * hd, bytes_accessed=seq * hd * 20, transcendentals=seq * seq // 2),
        name='attn_bwd',
    )(lmax, lim, lse, delta, q, do, k, kt, v)


def solution(mesh):
    size = mesh.shape['cp']
    seq_spec = P(('dp', 'cp'))
    part_spec = P('dp')
    rep_spec = P()

    def device_body(vis_loc, text_loc, img_pos, grad_y, pn_gain, w_proj, pre_gain, w_query, w_key, w_value, q_gain, k_gain, w_out, post_gain):
        rank = lax.axis_index('cp')
        even = rank % 2 == 0
        loc, dim = text_loc.shape
        seq = loc * size
        dim_v = vis_loc.shape[2]
        hd = q_gain.shape[0]
        heads = w_query.shape[1] // hd
        kv_heads = w_key.shape[1] // hd
        side = GRID // POOL
        block = side * side
        n_img = img_pos.shape[0]
        scale = hd ** -0.5
        bq = min(512, seq // 2)
        nq = seq // bq
        pn_f, pre_f, qg_f, kg_f, post_f = (g.astype(F32) for g in (pn_gain, pre_gain, q_gain, k_gain, post_gain))

        patch = jnp.arange(GRID * GRID)
        cell = (patch // (GRID * POOL)) * side + (patch % GRID) // POOL
        pool_mat = (jnp.arange(block)[:, None] == cell[None, :]).astype(BF)
        pooled = (mm(pool_mat, vis_loc[0]) / (POOL * POOL)).astype(BF)
        pooled_all = lax.all_gather(pooled, 'cp', tiled=True)

        pos_all = jnp.arange(seq)
        off_all = pos_all[:, None] - img_pos[None, :]
        in_all = (off_all >= 0) & (off_all < block)
        lim_all = jnp.where(jnp.any(in_all, axis=1), jnp.sum(jnp.where(in_all, img_pos[None, :] + block - 1, 0), axis=1), pos_all).astype(jnp.int32)
        lim = lim_all.reshape(nq, 1, bq)
        lmax = jnp.max(lim_all.reshape(nq, bq), axis=1)
        q_pos = rank * loc + jnp.arange(loc)
        offset = q_pos[:, None] - img_pos[None, :]
        in_blk = (offset >= 0) & (offset < block)
        is_img = jnp.any(in_blk, axis=1)
        flat_row = jnp.sum(jnp.where(in_blk, jnp.arange(n_img)[None, :] * block + offset, 0), axis=1)
        flat_row = jnp.where(is_img, flat_row, -1)
        img_mask = is_img[:, None]
        sel = (flat_row[:, None] == jnp.arange(n_img * block)[None, :]).astype(BF)

        pooled_rows = mm(sel, pooled_all).astype(BF)
        normed_rows, norm_pull = jax.vjp(gain_norm, pooled_rows, pn_f)
        soft_rows = mm(normed_rows, w_proj).astype(BF)
        merged = jnp.where(img_mask, soft_rows, text_loc)
        hidden, pre_pull = jax.vjp(gain_norm, merged, pre_f)
        hidden_all = lax.all_gather(hidden, 'cp', tiled=True)

        kv_id = rank * kv_heads // size
        wq_h = lax.dynamic_slice(w_query, (0, rank * hd), (dim, hd))
        wk_h = lax.dynamic_slice(w_key, (0, kv_id * hd), (dim, hd))
        wv_h = lax.dynamic_slice(w_value, (0, kv_id * hd), (dim, hd))
        wo_h = lax.dynamic_slice(w_out, (rank * hd, 0), (hd, dim))
        q_raw = mm(hidden_all, wq_h).astype(BF)
        k_raw = mm(hidden_all, wk_h).astype(BF)
        v = mm(hidden_all, wv_h).astype(BF)
        cos_t, sin_t = rope_tables(pos_all, hd)
        rot = functools.partial(head_rotate, cos_t=cos_t, sin_t=sin_t)
        q, q_pull = jax.vjp(rot, q_raw, qg_f)
        k, k_pull = jax.vjp(rot, k_raw, kg_f)
        qs = (q.astype(F32) * scale).astype(BF)

        o, o_wide, lse = attn_fwd(qs, k, v.T, lim, lmax, bq, block)
        o_rows = lax.all_to_all(o.reshape(size, loc, hd), 'cp', 0, 0, tiled=True)
        o_rows = o_rows.transpose(1, 0, 2).reshape(loc, heads * hd)
        proj_out = mm(o_rows, w_out).astype(BF)
        y_loc, post_pull = jax.vjp(post_residual, merged, proj_out, post_f)
        d_resid, d_proj, g_post = post_pull(grad_y)

        d_proj_all = lax.all_gather(d_proj, 'cp', tiled=True)
        d_o = mm(d_proj_all, wo_h, ((1,), (1,))).astype(BF)
        g_out_h = mm(o, d_proj_all, ((0,), (0,))).astype(BF)
        g_out = lax.all_gather(g_out_h, 'cp', tiled=True)
        delta = jnp.sum(d_o.astype(F32) * o_wide, axis=1).reshape(nq, 1, bq)
        d_q, d_k_part, d_v_part = attn_bwd(qs, k, k.T, v, d_o, lse, delta, lim, lmax, bq, block, scale)
        swap = [(i, i ^ 1) for i in range(size)]
        got = lax.ppermute(jnp.where(even, d_v_part, d_k_part), 'cp', swap)
        d_kv = (jnp.where(even, d_k_part, d_v_part) + got).astype(BF)
        d_q_raw, g_q_gain = q_pull(d_q)
        d_k_raw, g_k_gain = k_pull(d_kv)
        g_k_gain = jnp.where(even, g_k_gain, 0.0)
        d_head = jnp.concatenate([d_q_raw, jnp.where(even, d_k_raw, d_kv)], axis=1)
        d_rows = lax.all_to_all(d_head.reshape(size, loc, 2 * hd), 'cp', 0, 0, tiled=True)
        g_head = mm(hidden_all, d_head, ((0,), (0,))).astype(BF)
        g_head_all = lax.all_gather(g_head, 'cp')
        g_query = g_head_all[:, :, :hd].transpose(1, 0, 2).reshape(dim, heads * hd)
        g_key = g_head_all[0::2, :, hd:].transpose(1, 0, 2).reshape(dim, kv_heads * hd)
        g_value = g_head_all[1::2, :, hd:].transpose(1, 0, 2).reshape(dim, kv_heads * hd)

        d_q_flat = d_rows[:, :, :hd].transpose(1, 0, 2).reshape(loc, heads * hd)
        d_k_flat = d_rows[0::2, :, hd:].transpose(1, 0, 2).reshape(loc, kv_heads * hd)
        d_v_flat = d_rows[1::2, :, hd:].transpose(1, 0, 2).reshape(loc, kv_heads * hd)
        nt = ((1,), (1,))
        d_hidden = (mm(d_q_flat, w_query, nt) + mm(d_k_flat, w_key, nt) + mm(d_v_flat, w_value, nt)).astype(BF)
        d_merged_attn, g_pre = pre_pull(d_hidden)
        d_merged = (d_resid.astype(F32) + d_merged_attn.astype(F32)).astype(BF)
        zero = jnp.zeros((), BF)
        grad_text = jnp.where(img_mask, zero, d_merged)
        d_soft = jnp.where(img_mask, d_merged, zero)
        d_normed = mm(d_soft, w_proj, nt).astype(BF)
        d_pooled_rows, g_pn = norm_pull(d_normed)
        d_pooled_all = mm(sel, d_pooled_rows, ((0,), (0,))).astype(BF)
        d_pooled = lax.psum_scatter(d_pooled_all, 'cp', scatter_dimension=0, tiled=True)
        spread = (d_pooled.astype(F32) / (POOL * POOL)).astype(BF)
        grad_vis = mm(pool_mat, spread, ((0,), (0,))).astype(BF)[None]

        g_proj_part = mm(normed_rows, d_soft, ((0,), (0,)))
        g_proj_loc = lax.psum_scatter(g_proj_part, 'cp', scatter_dimension=0, tiled=True).astype(BF)
        g_proj = lax.all_gather(g_proj_loc, 'cp', tiled=True)
        small = lax.psum(jnp.concatenate([g_pn, g_pre, g_q_gain, g_k_gain, g_post]), 'cp').astype(BF)
        edges = [0, dim_v, dim_v + dim, dim_v + dim + hd, dim_v + dim + 2 * hd, dim_v + 2 * dim + 2 * hd]
        s_pn, s_pre, s_q, s_k, s_post = (small[a:b] for a, b in zip(edges[:-1], edges[1:]))
        return y_loc, grad_text, grad_vis, s_pn, g_proj, s_pre, g_query, g_key, g_value, s_q, s_k, g_out, s_post

    in_specs = (seq_spec, seq_spec, part_spec, seq_spec) + (rep_spec,) * 10
    out_specs = (seq_spec, seq_spec, seq_spec) + (part_spec,) * 10
    return jax.shard_map(device_body, mesh=mesh, in_specs=in_specs, out_specs=out_specs, check_vma=False)
```

time: 1410 us -> 944 us (0.67)
  blocking collectives: 667 us -> 75.8 us
  waiting for transfers between devices: 88.8 us -> 409 us
  matrix products: 392 us -> 144 us
  Pallas kernels: 0 us -> 83 us
  other arithmetic: 143 us -> 116 us
    psum x1, blocking collectives: 667 us -> 23 us  [device_body(): lax.psum(jnp.concatenate([g_pn, g_pre, g_q_gain, g_k_gain, g_post]), 'cp')]
    all_gather x3 -> x6, waiting for transfers between devices: 50.2 us -> 329 us  [the longest x1 90.2 us: device_body(): d_proj_all = lax.all_gather(d_proj, 'cp', tiled=True)]
    dot_general x21 -> x17, matrix products: 392 us -> 144 us  [mm(): return lax.dot_general(a, b, (dims, ((), ())), preferred_element_type=F32)]
    pallas_call x0 -> x2, Pallas kernels: none -> 83 us  [the longest x1 46.3 us: attn_bwd(): pl.pallas_call(body, out_shape=(jax.ShapeDtypeStruct((seq, hd), BF), jax....]
    sub x1, other arithmetic: 66.6 us -> 0.01 us  [device_body(): img_pos[None, :] + block - 1]
    all_to_all x0 -> x1, blocking collectives: none -> 52.9 us  [device_body(): lax.all_to_all(d_head.reshape(size, loc, 2 * hd), 'cp', 0, 0, tiled=True)]
    reduce_sum x3, other arithmetic: 11.2 us -> 41.4 us  [rms_scale(): return wide_vals * lax.rsqrt(mean_sq + EPS) * (1.0 + gain_vec)]
    all_to_all x0 -> x1, waiting for transfers between devices: none -> 26.2 us  [device_body(): o_rows = lax.all_to_all(o.reshape(size, loc, hd), 'cp', 0, 0, tiled=True)]
  transfers between devices with their start and end apart: 6 -> 10, of which waited for: 3 -> 9; matrix products, arithmetic and copies ran while one was open for 24% -> 11% of each run, Pallas kernels for 0% -> 0%
where the time goes in v1:
time: 944 us; the launch traced here: 937 us
  waiting for transfers between devices  409 us (43%)
  matrix products  144 us (15%)
  other arithmetic  116 us (12%)
  local copies, waits for them, and re-layouts  88.6 us (9%)
  Pallas kernels  83 us (9%)
  blocking collectives  75.8 us (8%)
  between operations  15.3 us (2%)
    dot_general x17, matrix products, mm(): return lax.dot_general(a, b, (dims, ((), ())), preferred_element_type=F32)  144 us
    all_gather x1, waiting for transfers between devices, device_body(): d_proj_all = lax.all_gather(d_proj, 'cp', tiled=True)  90.2 us
    all_gather x1, waiting for transfers between devices, device_body(): hidden_all = lax.all_gather(hidden, 'cp', tiled=True)  89.4 us
    all_gather x1, waiting for transfers between devices, device_body(): g_head_all = lax.all_gather(g_head, 'cp')  87.5 us
    all_to_all x1, blocking collectives, device_body(): lax.all_to_all(d_head.reshape(size, loc, 2 * hd), 'cp', 0, 0, tiled=True)  52.9 us
    pallas_call x1, Pallas kernels, attn_bwd(): pl.pallas_call(body, out_shape=(jax.ShapeDtypeStruct((seq, hd), BF), jax....  46.3 us
    reduce_sum x3, other arithmetic, rms_scale(): return wide_vals * lax.rsqrt(mean_sq + EPS) * (1.0 + gain_vec)  41.4 us
    unnamed x117, local copies, waits for them, and re-layouts  40.8 us
  transfers between devices with their start and end apart: 10, of which 9 were waited for; matrix products, arithmetic and copies ran while one was open for 11% of the time, Pallas kernels for 0%

profile of v1, /device:TPU:113, one launch (start us, length us, event | category | flops | bytes accessed | tf_op | source)
XLA Modules:
  0.0 937.4 jit_solution(3290593595215888816)
XLA Ops:
  7.9 7.5 fusion.54
  15.9 32.9 %all-gather.8.cloned.1.call-done = bf16[2048,1152]{1,0:T(8,128)(2,1)} async-done(((bf16[256,1152]{1,0:T(8,128)(2,1)}), bf16[2048,1152]{1,0:T(8,128)(2,1)}) %all-gather.8.cloned.1.call-update) | async-done | bytes 4718608 | tf_op jit(solution)/shard_map/all_gather | solution.py:207
  54.8 6.7 fusion.19
  65.9 89.4 %all-gather.10.cloned.1.call-done = bf16[4096,2304]{1,0:T(8,128)(2,1)} async-done(((bf16[512,2304]{1,0:T(8,128)(2,1)}), bf16[4096,2304]{1,0:T(8,128)(2,1)}) %all-gather.10.cloned.1.call-update) | async-done | bytes 18874384 | tf_op jit(solution)/shard_map/all_gather | solution.py:229
  155.3 10.3 %convolution_convert_fusion.3.v_ref = bf16[4096,256]{1,0:T(8,128)(2,1)} fusion(bf16[4096,2304]{1,0:T(8,128)(2,1)} %all-gather.10.cloned.1.call-done, bf16[2304,1024]{1,0:T(8,128)(2,1)} %param.23, s32[]{:T(128)S(6)} %select_n.129), kind=kOutput, calls=%fused_computation.41 | convolution fusion | flops 4832886784 | bytes 22151172 | tf_op jit(solution)/shard_map/dot_general | solution.py:51
  169.7 9.4 %fusion.33 = (f32[4096]{0:T(1024)S(1)}, bf16[4096,256]{0,1:T(8,128)(2,1)S(1)}) fusion(bf16[4096,2304]{1,0:T(8,128)(2,1)} %all-gather.10.cloned.1.call-done, bf16[2304,1024]{1,0:T(8,128)(2,1)} %param.22, s32[]{:T(128)S(6)} %select_n.129), kind=kOutput, calls=%fused_computation.77 | convolution fusion | flops 4836028416 | bytes 22167556 | tf_op jit(solution)/shard_map/dot_general | solution.py:51
  179.1 10.4 %fusion.31 = (f32[4096]{0:T(1024)S(1)}, bf16[4096,256]{0,1:T(8,128)(2,1)S(1)}) fusion(bf16[4096,2304]{1,0:T(8,128)(2,1)} %all-gather.10.cloned.1.call-done, bf16[2304,2048]{1,0:T(8,128)(2,1)} %param.21, s32[]{:T(128)S(6)} %select_n.127), kind=kOutput, calls=%fused_computation.75 | convolution fusion | flops 4836028416 | bytes 22167556 | tf_op jit(solution)/shard_map/dot_general | solution.py:51
  193.5 20.7 %fusion.44 = (bf16[4096,256]{0,1:T(8,128)(2,1)}, bf16[4096,256]{0,1:T(8,128)(2,1)}) fusion(f32[4096,128]{0,1:T(8,128)S(1)} %broadcast_multiply_fusion, f32[4096,128]{0,1:T(8,128)S(1)} %get-tuple-element.48, f32[4096,128]{0,1:T(8,128)S(1)} %get-tuple-element.47, f32[256]{0:T(256)S(1)} %convert_add_fusion.5, f32[4096]{0:T(1024)S(1)} %fusion.102, ...), kind=kLoop, calls=%fused_computation.90 | loop fusion | flops 20971520 | bytes 18909184 | tf_op jit(solution)/shard_map/jvp()/convert_element_type | solution.py:43
  222.5 36.7 %attn_fwd.1 = (bf16[4096,256]{1,0:T(8,128)(2,1)S(1)}, f32[4096,256]{1,0:T(8,128)}, f32[8,1,512]{2,1,0:T(1,128)S(1)}) custom-call(s32[8]{0:T(128)S(1)} %select_reduce_fusion.1.lmax_ref, s32[8,1,512]{2,1,0:T(1,128)S(1)} %add_select_fusion.2.lim_ref, bf16[4096,256]{1,0:T(8,128)(2,1)S(1)} %copy-done, bf16[4096,256]{1,0:T(8,128)(2,1)} %copy.60.k_ref, ...), custom_call_target="tpu_custom_call" | custom-call | flops 8589934592 | bytes 14680064 | tf_op jit(solution)/shard_map/attn_fwd/pallas_call | solution.py:99
  266.7 26.2 %all-to-all-done = bf16[8,512,256]{1,2,0:T(8,128)(2,1)} async-done(((bf16[8,512,256]{1,2,0:T(8,128)(2,1)}), bf16[8,512,256]{1,2,0:T(8,128)(2,1)}, u32[]{:S(2)}, u32[]{:S(2)}) %all-to-all-start) | async-done | bytes 2097184 | tf_op jit(solution)/shard_map/all_to_all | solution.py:246
  292.8 9.6 %fusion.17 = (f32[512]{0:T(512)S(1)}, bf16[512,2304]{1,0:T(8,128)(2,1)S(1)}) fusion(bf16[512,2048]{0,1:T(8,128)(2,1)} %bitcast.5, bf16[2048,2304]{1,0:T(8,128)(2,1)} %param.26), kind=kOutput, calls=%fused_computation.56 | convolution fusion | flops 4836556288 | bytes 13895680 | tf_op jit(solution)/shard_map/dot_general | solution.py:51
  308.8 90.2 %all-gather.12.cloned.1.call-done = bf16[4096,2304]{1,0:T(8,128)(2,1)} async-done(((bf16[512,2304]{1,0:T(8,128)(2,1)}), bf16[4096,2304]{1,0:T(8,128)(2,1)}) %all-gather.12.cloned.1.call-update) | async-done | bytes 18874384 | tf_op jit(solution)/shard_map/all_gather | solution.py:252
  399.0 12.5 %multiply_reduce_fusion = (f32[4096]{0:T(1024)}, bf16[4096,256]{1,0:T(8,128)(2,1)}) fusion(f32[4096,256]{1,0:T(8,128)} %get-tuple-element.21, bf16[4096,2304]{1,0:T(8,128)(2,1)} %all-gather.12.cloned.1.call-done, bf16[2048,2304]{1,0:T(8,128)(2,1)} %param.26, s32[]{:T(128)S(6)} %select_n.127), kind=kOutput, calls=%fused_computation.93 | convolution fusion | flops 4836028416 | bytes 26361860 | tf_op jit(solution)/shard_map/dot_general | solution.py:51
  411.5 46.3 %attn_bwd.1 = (bf16[4096,256]{1,0:T(8,128)(2,1)}, f32[4096,256]{1,0:T(8,128)}, f32[4096,256]{1,0:T(8,128)}) custom-call(s32[8]{0:T(128)} %copy-done.2, s32[8,1,512]{2,1,0:T(1,128)} %copy-done.1, f32[8,1,512]{2,1,0:T(1,128)} %copy-done.3, f32[8,1,512]{2,1,0:T(1,128)} %bitcast.79, bf16[4096,256]{1,0:T(8,128)(2,1)} %copy.59.q_ref, ...), custom_call_target="tpu_custom_call" | custom-call | flops 21474836480 | bytes 20971520 | tf_op jit(solution)/shard_map/attn_bwd/pallas_call | solution.py:164
  478.2 15.0 %convert_multiply_fusion.22 = f32[4096,256]{0,1:T(8,128)S(1)} fusion(bf16[4096,256]{0,1:T(8,128)(2,1)} %copy.66, f32[4096,128]{0,1:T(8,128)} %copy-done.4), kind=kLoop, calls=%fused_computation.38 | loop fusion | flops 3145728 | bytes 8388608 | tf_op jit(solution)/shard_map/transpose(jvp())/mul | solution.py:39
  496.7 20.4 %fusion.24 = (f32[256]{0:T(256)S(1)}, f32[4096]{0:T(1024)S(1)}, f32[4096,256]{0,1:T(8,128)S(1)}, bf16[4096,256]{0,1:T(8,128)(2,1)S(1)}) fusion(bf16[4096,256]{0,1:T(8,128)(2,1)S(1)} %copy-done.11, f32[4096]{0:T(1024)S(1)} %fusion.101, f32[4096,128]{0,1:T(8,128)S(1)} %get-tuple-element.44, f32[4096,128]{0,1:T(8,128)S(1)} %get-tuple-element.43, ...), kind=kLoop, calls=%fused_computation.68 | loop fusion | flops 17821440 | bytes 29394944 | tf_op jit(solution)/shard_map/transpose(jvp())/reduce_sum | solution.py:22
  518.7 18.7 %fusion.23 = (f32[256]{0:T(256)S(1)}, f32[4096]{0:T(1024)S(1)}, bf16[4096,256]{0,1:T(8,128)(2,1)S(1)}) fusion(bf16[4096,256]{0,1:T(8,128)(2,1)S(1)} %copy-done.9, f32[4096]{0:T(1024)S(1)} %fusion.102, f32[4096,128]{0,1:T(8,128)S(1)} %get-tuple-element.46, f32[4096,128]{0,1:T(8,128)S(1)} %get-tuple-element.45, f32[4096,128]{0,1:T(8,128)S(1)} %copy-done.5, ...), kind=kLoop, calls=%fused_computation.67 | loop fusion | flops 24112896 | bytes 21040128 | tf_op jit(solution)/shard_map/transpose(jvp())/reduce_sum | solution.py:22
  537.5 16.8 %fusion.62 = bf16[4096,256]{0,1:T(8,128)(2,1)S(1)} fusion(bf16[4096,256]{0,1:T(8,128)(2,1)S(1)} %get-tuple-element.55, bf16[4096,256]{0,1:T(8,128)(2,1)S(1)} %copy-done.9, f32[4096]{0:T(1024)S(1)} %multiply_multiply_fusion, f32[256]{0:T(256)S(1)} %convert_add_fusion.5, f32[4096]{0:T(1024)S(1)} %fusion.102, pred[]{:T(512)S(6)} %eq.45, ...), kind=kLoop, calls=%fused_computation.119 | loop fusion | flops 13631488 | bytes 12616705 | tf_op jit(solution)/shard_map/jit(_where)/select_n | solution.py:264
  556.0 52.9 %all_to_all.10 = bf16[8,512,512]{1,2,0:T(8,128)(2,1)S(1)} all-to-all(bf16[8,512,512]{1,2,0:T(8,128)(2,1)S(1)} %bitcast.64), channel_id=1, replica_groups=mesh['dp'=2,'cp'=8] {'cp'}, dimensions={0} | all-to-all | bytes 8388608 | tf_op jit(solution)/shard_map/all_to_all | solution.py:265
  613.8 11.5 %convolution_add_fusion = f32[512,2304]{1,0:T(8,128)} fusion(f32[512,2304]{1,0:T(8,128)} %fusion.120, bf16[512,2048]{0,1:T(8,128)(2,1)S(1)} %bitcast.71, bf16[2304,2048]{1,0:T(8,128)(2,1)} %param.21), kind=kOutput, calls=%fused_computation.48 | convolution fusion | flops 4833017856 | bytes 20971520 | tf_op jit(solution)/shard_map/dot_general | solution.py:51
  642.3 10.1 %convolution_convert_fusion.9 = bf16[256,2304]{1,0:T(8,128)(2,1)} fusion(bf16[4096,256]{1,0:T(8,128)(2,1)S(1)} %get-tuple-element.19, bf16[4096,2304]{1,0:T(8,128)(2,1)} %all-gather.12.cloned.1.call-done), kind=kOutput, calls=%fused_computation.103 | convolution fusion | flops 4832428032 | bytes 22151168 | tf_op jit(solution)/shard_map/dot_general | solution.py:51
  652.8 6.7 fusion.58
  666.3 15.6 %convolution_convert_fusion.8 = bf16[2304,512]{1,0:T(8,128)(2,1)} fusion(bf16[4096,2304]{1,0:T(8,128)(2,1)} %all-gather.10.cloned.1.call-done, bf16[4096,256]{0,1:T(8,128)(2,1)S(1)} %copy-done.20, bf16[4096,256]{0,1:T(8,128)(2,1)} %copy-done.21), kind=kOutput, calls=%fused_computation.66 | convolution fusion | flops 9673244672 | bytes 25427968 | tf_op jit(solution)/shard_map/dot_general | solution.py:51
  682.1 18.7 %reduce-scatter.5.cloned.1.call-done = f32[144,2304]{1,0:T(8,128)} async-done(((f32[1152,2304]{1,0:T(8,128)}), f32[144,2304]{1,0:T(8,128)}) %reduce-scatter.5.cloned.1.call-update) | async-done | bytes 1327120 | tf_op jit(solution)/shard_map/reduce_scatter | solution.py:290
  703.2 23.0 %psum.7 = bf16[6272]{0:T(1024)(128)(2,1)S(1)} all-reduce(f32[6272]{0:T(1024)S(1)} %constant_dynamic-update-slice_fusion), channel_id=1, replica_groups=mesh['dp'=2,'cp'=8] {'cp'}, use_global_device_ids=true, to_apply=%region_22.23 | all-reduce | flops 6272 | bytes 37632 | tf_op jit(solution)/shard_map/psum | solution.py:292
  727.9 25.6 %all-gather.16.cloned.1.call-done = bf16[2048,2304]{1,0:T(8,128)(2,1)} async-done(((bf16[256,2304]{1,0:T(8,128)(2,1)}), bf16[2048,2304]{1,0:T(8,128)(2,1)}) %all-gather.16.cloned.1.call-update) | async-done | bytes 9437200 | tf_op jit(solution)/shard_map/all_gather | solution.py:255
  753.5 34.7 %reduce-scatter.3.cloned.1.call-done = bf16[256,1152]{1,0:T(8,128)(2,1)} async-done(((bf16[2048,1152]{1,0:T(8,128)(2,1)}), bf16[256,1152]{1,0:T(8,128)(2,1)}) %reduce-scatter.3.cloned.1.call-update) | async-done | bytes 589840 | tf_op jit(solution)/shard_map/reduce_scatter | solution.py:285
  788.2 6.9 fusion
  795.1 87.5 %all-gather.18.cloned.1.call-done = bf16[18432,512]{1,0:T(8,128)(2,1)} async-done(((bf16[2304,512]{1,0:T(8,128)(2,1)}), bf16[18432,512]{1,0:T(8,128)(2,1)}) %all-gather.18.cloned.1.call-update) | async-done | bytes 18874384 | tf_op jit(solution)/shard_map/all_gather | solution.py:267
  892.1 8.0 slice_bitcast_fusion
  900.1 8.8 copy.77
  922.4 8.0 copy.90
  (204 shorter events, 124.5 us)
Async XLA Ops:
  7.2 41.6 %all-gather.8.cloned.1.call-start = ((), (), s32[]{:S(2)}) async-start(), calls=%async_computation.4 | async-start | bytes 5308416 | tf_op jit(solution)/shard_map/all_gather | solution.py:207
  15.5 139.8 %all-gather.10.cloned.1.call-start = ((), (), s32[]{:S(2)}) async-start(), calls=%async_computation.5 | async-start | bytes 21233664 | tf_op jit(solution)/shard_map/all_gather | solution.py:229
  15.7 39.1 %copy-start.39 = (pred[512]{0:T(512)(128)(4,1)}, pred[512]{0:T(512)(128)(4,1)S(1)}, u32[]{:S(2)}) copy-start(pred[512]{0:T(512)(128)(4,1)S(1)} %fusion.103) | copy-start | bytes 1540
  15.8 38.4 %copy-start.42 = (s32[512]{0:T(512)}, s32[512]{0:T(512)S(1)}, u32[]{:S(2)}) copy-start(s32[512]{0:T(512)S(1)} %broadcast_select_fusion.5) | copy-start | bytes 6148
  15.8 39.0 %copy-start.35 = (f32[1152]{0:T(1024)}, f32[1152]{0:T(1024)S(1)}, u32[]{:S(2)}) copy-start(f32[1152]{0:T(1024)S(1)} %convert_add_fusion.4) | copy-start | bytes 13828
  15.8 46.3 %copy-start.23 = (f32[2304]{0:T(1024)}, f32[2304]{0:T(1024)S(1)}, u32[]{:S(2)}) copy-start(f32[2304]{0:T(1024)S(1)} %convert_add_fusion.3) | copy-start | bytes 27652
  15.9 39.0 %copy-start.46 = (bf16[512,2304]{1,0:T(8,128)(2,1)S(1)}, bf16[512,2304]{1,0:T(8,128)(2,1)}, u32[]{:S(2)}) copy-start(bf16[512,2304]{1,0:T(8,128)(2,1)} %param.15) | copy-start | bytes 7077892
  65.6 155.3 %copy-start.2 = (s32[8]{0:T(128)}, s32[8]{0:T(128)S(1)}, u32[]{:S(2)}) copy-start(s32[8]{0:T(128)S(1)} %select_reduce_fusion.1.lmax_ref) | copy-start | bytes 100
  65.6 155.2 %copy-start.1 = (s32[8,1,512]{2,1,0:T(1,128)}, s32[8,1,512]{2,1,0:T(1,128)S(1)}, u32[]{:S(2)}) copy-start(s32[8,1,512]{2,1,0:T(1,128)S(1)} %add_select_fusion.2.lim_ref) | copy-start | bytes 49156
  65.9 127.6 %copy-start.4 = (f32[4096,128]{0,1:T(8,128)}, f32[4096,128]{0,1:T(8,128)S(1)}, u32[]{:S(2)}) copy-start(f32[4096,128]{0,1:T(8,128)S(1)} %broadcast_multiply_fusion) | copy-start | bytes 6291460
  179.1 14.4 %copy-start.8 = (bf16[4096,256]{0,1:T(8,128)(2,1)}, bf16[4096,256]{0,1:T(8,128)(2,1)S(1)}, u32[]{:S(2)}) copy-start(bf16[4096,256]{0,1:T(8,128)(2,1)S(1)} %get-tuple-element.67) | copy-start | bytes 6291460
  262.1 30.7 %all-to-all-start = ((bf16[8,512,256]{1,2,0:T(8,128)(2,1)}), bf16[8,512,256]{1,2,0:T(8,128)(2,1)}, u32[]{:S(2)}, u32[]{:S(2)}) async-start(bf16[8,512,256]{1,2,0:T(8,128)(2,1)} %copy.62), calls=%async_computation | async-start | bytes 4194304 | tf_op jit(solution)/shard_map/all_to_all | solution.py:246
  266.6 132.4 %all-gather.12.cloned.1.call-start = ((), (), s32[]{:S(2)}) async-start(), calls=%async_computation.6 | async-start | bytes 21233664 | tf_op jit(solution)/shard_map/all_gather | solution.py:252
  292.8 9.6 %copy-start.16 = (bf16[512,2304]{1,0:T(8,128)(2,1)S(1)}, bf16[512,2304]{1,0:T(8,128)(2,1)}, u32[]{:S(2)}) copy-start(bf16[512,2304]{1,0:T(8,128)(2,1)} %param.17) | copy-start | bytes 7077892
  308.7 392.1 %reduce-scatter.5.cloned.1.call-start = ((), (), s32[]{:S(2)}) async-start(), calls=%async_computation.8 | async-start | bytes 11943936 | tf_op jit(solution)/shard_map/reduce_scatter | solution.py:290
  473.9 19.7 %collective-permute-start = (f32[4096,256]{0,1:T(8,128)}, f32[4096,256]{0,1:T(8,128)}, u32[]{:S(2)}, u32[]{:S(2)}) collective-permute-start(f32[4096,256]{0,1:T(8,128)} %broadcast_select_fusion.2), channel_id=1, source_target_pairs={{0,1},{1,0},{2,3},{3,2},{4,5},{5,4},{6,7},{7,6},{8,9},{9,8},{10,11... | collective-permute-start | bytes 12582920 | tf_op jit(solution)/shard_map/ppermute | solution.py:259
  478.2 15.4 %copy-start.7 = (f32[4096,256]{0,1:T(8,128)S(1)}, f32[4096,256]{0,1:T(8,128)}, u32[]{:S(2)}) copy-start(f32[4096,256]{0,1:T(8,128)} %copy.68) | copy-start | bytes 12582916
  478.2 15.4 %copy-start.12 = (bf16[4096,256]{0,1:T(8,128)(2,1)S(1)}, bf16[4096,256]{0,1:T(8,128)(2,1)}, u32[]{:S(2)}) copy-start(bf16[4096,256]{0,1:T(8,128)(2,1)} %copy.66) | copy-start | bytes 6291460
  537.5 16.8 %copy-start.21 = (bf16[4096,256]{0,1:T(8,128)(2,1)}, bf16[4096,256]{0,1:T(8,128)(2,1)S(1)}, u32[]{:S(2)}) copy-start(bf16[4096,256]{0,1:T(8,128)(2,1)S(1)} %get-tuple-element.53) | copy-start | bytes 6291460
  555.6 53.5 %slice-start = ((s8[4718592]{0:T(1024)(128)(4,1)}), s8[4194304]{0:T(1024)(128)(4,1)S(1)}, s32[]{:S(2)}) async-start(s8[4718592]{0:T(1024)(128)(4,1)} %bitcast.75), calls=%async_computation.12 | async-start | bytes 8388608
  556.0 53.1 %slice-start.1 = ((s8[4718592]{0:T(1024)(128)(4,1)}), s8[524288]{0:T(1024)(128)(4,1)S(1)}, s32[]{:S(2)}) async-start(s8[4718592]{0:T(1024)(128)(4,1)} %bitcast.75), calls=%async_computation.13 | async-start | bytes 1048576
  609.1 16.1 %slice-start.2 = ((s8[4718592]{0:T(1024)(128)(4,1)}), s8[524288]{0:T(1024)(128)(4,1)S(1)}, s32[]{:S(2)}) async-start(s8[4718592]{0:T(1024)(128)(4,1)} %bitcast.77), calls=%async_computation.14 | async-start | bytes 1048576
  613.7 11.5 %copy-start.15 = (bf16[512,2304]{1,0:T(8,128)(2,1)S(1)}, bf16[512,2304]{1,0:T(8,128)(2,1)}, u32[]{:S(2)}) copy-start(bf16[512,2304]{1,0:T(8,128)(2,1)} %copy-done.13) | copy-start | bytes 7077892
  613.7 11.5 %copy-start.24 = (f32[2304]{0:T(1024)S(1)}, f32[2304]{0:T(1024)}, u32[]{:S(2)}) copy-start(f32[2304]{0:T(1024)} %copy-done.23) | copy-start | bytes 27652
  613.8 11.5 %copy-start.29 = (f32[512]{0:T(512)S(1)}, f32[512]{0:T(512)}, u32[]{:S(2)}) copy-start(f32[512]{0:T(512)} %copy-done.28) | copy-start | bytes 6148
  613.8 11.5 %slice-start.3 = ((s8[4718592]{0:T(1024)(128)(4,1)}), s8[4194304]{0:T(1024)(128)(4,1)S(1)}, s32[]{:S(2)}) async-start(s8[4718592]{0:T(1024)(128)(4,1)} %bitcast.77), calls=%async_computation.15 | async-start | bytes 8388608
  642.2 111.3 %all-gather.16.cloned.1.call-start = ((), (), s32[]{:S(2)}) async-start(), calls=%async_computation.10 | async-start | bytes 10616832 | tf_op jit(solution)/shard_map/all_gather | solution.py:255
  652.5 135.7 %reduce-scatter.3.cloned.1.call-start = ((), (), s32[]{:S(2)}) async-start(), calls=%async_computation.7 | async-start | bytes 5308416 | tf_op jit(solution)/shard_map/reduce_scatter | solution.py:285
  664.8 217.8 %all-gather.18.cloned.1.call-start = ((), (), s32[]{:S(2)}) async-start(), calls=%async_computation.11 | async-start | bytes 21233664 | tf_op jit(solution)/shard_map/all_gather | solution.py:267
  682.0 21.2 %copy-start.27 = (f32[2304]{0:T(1024)S(1)}, f32[2304]{0:T(1024)}, u32[]{:S(2)}) copy-start(f32[2304]{0:T(1024)} %get-tuple-element.29) | copy-start | bytes 27652
  682.0 106.2 %copy-start.26 = (s32[4096]{0:T(1024)S(1)}, s32[4096]{0:T(1024)}, u32[]{:S(2)}) copy-start(s32[4096]{0:T(1024)} %copy-done.25) | copy-start | bytes 49156
  682.0 235.2 %all-gather.14.cloned.1.call-start = ((), (), s32[]{:S(2)}) async-start(), calls=%async_computation.9 | async-start | bytes 5971968 | tf_op jit(solution)/shard_map/all_gather | solution.py:291
  (33 other events, 129.0 us)
Sparse Core Ops, SparseCore 0:
  15.6 33.1 all-gather.7
  65.2 90.0 all-gather.9
  308.8 90.1 all-gather.11
  642.3 58.4 reduce-scatter.4
  702.8 50.6 all-gather.15
  756.2 31.9 reduce-scatter.2
  790.3 92.2 all-gather.17
  884.2 32.9 all-gather.13

commit v2 on v1

--- a/solution.py
+++ b/solution.py
@@ -29,18 +29,7 @@
 def rope_tables(positions, head_dim):
     inv_freq = ROPE_BASE ** (-jnp.arange(0, head_dim, 2).astype(F32) / head_dim)
     rot_angle = (positions.astype(F32) / ROPE_SCALE)[:, None] * inv_freq[None, :]
-    rot_angle = jnp.concatenate([rot_angle, rot_angle], axis=-1)
     return jnp.cos(rot_angle), jnp.sin(rot_angle)
-
-
-def apply_rope(values, cos_t, sin_t):
-    half_dim = values.shape[-1] // 2
-    rotated = jnp.concatenate([-values[..., half_dim:], values[..., :half_dim]], axis=-1)
-    return values * cos_t + rotated * sin_t
-
-
-def head_rotate(raw, gain, cos_t, sin_t):
-    return apply_rope(rms_scale(raw, gain), cos_t, sin_t).astype(BF)
 
 
 def post_residual(merged, proj_out, gain_vec):
@@ -112,7 +101,7 @@
     )(lmax, lim, q, k, vt)
 
 
-def attn_bwd_body(lmax_ref, lim_ref, lse_ref, dl_ref, q_ref, do_ref, k_ref, kt_ref, v_ref, dq_ref, dk_ref, dv_ref, acc_ref, *, bq, bo, scale):
+def attn_bwd_body(lmax_ref, even_ref, lim_ref, lse_ref, dl_ref, q_ref, do_ref, k_ref, kt_ref, v_ref, dq_ref, keep_ref, send_ref, acc_ref, dk_ref, dv_ref, *, bq, bo, scale):
     qi = pl.program_id(0)
     q0 = qi * bq
 
@@ -152,29 +141,143 @@
         tile(pl.multiple_of(q0 + bq, bq), bo, True)
 
     dq_ref[...] = (jnp.transpose(acc_ref[...]) * scale).astype(BF)
-
-
-def attn_bwd(q, k, kt, v, do, lse, delta, lim, lmax, bq, bo, scale):
+    last = qi == pl.num_programs(0) - 1
+
+    @pl.when(last & (even_ref[0] == 1))
+    def _():
+        keep_ref[...] = dk_ref[...]
+        send_ref[...] = dv_ref[...]
+
+    @pl.when(last & (even_ref[0] == 0))
+    def _():
+        keep_ref[...] = dv_ref[...]
+        send_ref[...] = dk_ref[...]
+
+
+def attn_bwd(q, k, kt, v, do, lse, delta, lim, lmax, even, bq, bo, scale):
     seq, hd = q.shape
     nq = seq // bq
     body = functools.partial(attn_bwd_body, bq=bq, bo=bo, scale=scale)
-    row = pl.BlockSpec((1, 1, bq), lambda i, s: (i, 0, 0))
-    tile = pl.BlockSpec((bq, hd), lambda i, s: (i, 0))
-    whole = pl.BlockSpec((seq, hd), lambda i, s: (0, 0))
+    row = pl.BlockSpec((1, 1, bq), lambda i, s, e: (i, 0, 0))
+    tile = pl.BlockSpec((bq, hd), lambda i, s, e: (i, 0))
+    whole = pl.BlockSpec((seq, hd), lambda i, s, e: (0, 0))
     return pl.pallas_call(
         body,
         out_shape=(jax.ShapeDtypeStruct((seq, hd), BF), jax.ShapeDtypeStruct((seq, hd), F32), jax.ShapeDtypeStruct((seq, hd), F32)),
         grid_spec=pltpu.PrefetchScalarGridSpec(
-            num_scalar_prefetch=1,
+            num_scalar_prefetch=2,
             grid=(nq,),
-            in_specs=[row, row, row, tile, tile, whole, pl.BlockSpec((hd, seq), lambda i, s: (0, 0)), whole],
+            in_specs=[row, row, row, tile, tile, whole, pl.BlockSpec((hd, seq), lambda i, s, e: (0, 0)), whole],
             out_specs=(tile, whole, whole),
-            scratch_shapes=[pltpu.VMEM((hd, bq), F32)],
+            scratch_shapes=[pltpu.VMEM((hd, bq), F32), pltpu.VMEM((seq, hd), F32), pltpu.VMEM((seq, hd), F32)],
         ),
         compiler_params=pltpu.CompilerParams(dimension_semantics=('arbitrary',), vmem_limit_bytes=56 * 1024 * 1024),
         cost_estimate=pl.CostEstimate(flops=5 * seq * seq * hd, bytes_accessed=seq * hd * 20, transcendentals=seq * seq // 2),
         name='attn_bwd',
-    )(lmax, lim, lse, delta, q, do, k, kt, v)
+    )(lmax, even, lim, lse, delta, q, do, k, kt, v)
+
+
+def turn(y, cos_t, sin_t):
+    half = y.shape[1] // 2
+    lo, hi = y[:, :half], y[:, half:]
+    return jnp.concatenate([lo * cos_t - hi * sin_t, hi * cos_t + lo * sin_t], axis=1)
+
+
+def turn_back(d, cos_t, sin_t):
+    half = d.shape[1] // 2
+    lo, hi = d[:, :half], d[:, half:]
+    return jnp.concatenate([lo * cos_t + hi * sin_t, hi * cos_t - lo * sin_t], axis=1)
+
+
+def qkv_body(h_ref, w_ref, cos_ref, sin_ref, qg_ref, kg_ref, qr_ref, kr_ref, q_ref, k_ref, kt_ref, v_ref, vt_ref, *, hd, scale):
+    acc = mm(h_ref[...], w_ref[...])
+    cos_t, sin_t = cos_ref[...], sin_ref[...]
+    q_raw = acc[:, :hd].astype(BF)
+    k_raw = acc[:, hd:2 * hd].astype(BF)
+    v = acc[:, 2 * hd:].astype(BF)
+    qr_ref[...] = q_raw
+    kr_ref[...] = k_raw
+    v_ref[...] = v
+    vt_ref[...] = jnp.transpose(v.astype(F32)).astype(BF)
+    q = turn(rms_scale(q_raw, qg_ref[...]), cos_t, sin_t).astype(BF)
+    q_ref[...] = (q.astype(F32) * scale).astype(BF)
+    k = turn(rms_scale(k_raw, kg_ref[...]), cos_t, sin_t).astype(BF)
+    k_ref[...] = k
+    kt_ref[...] = jnp.transpose(k.astype(F32)).astype(BF)
+
+
+def qkv_call(h, w, cos_t, sin_t, qg, kg, bm, scale):
+    seq, dim = h.shape
+    hd = w.shape[1] // 3
+    tile = pl.BlockSpec((bm, hd), lambda i: (i, 0))
+    tall = pl.BlockSpec((hd, bm), lambda i: (0, i))
+    table = pl.BlockSpec((bm, hd // 2), lambda i: (i, 0))
+    gain = pl.BlockSpec((1, hd), lambda i: (0, 0))
+    flat = jax.ShapeDtypeStruct((seq, hd), BF)
+    high = jax.ShapeDtypeStruct((hd, seq), BF)
+    return pl.pallas_call(
+        functools.partial(qkv_body, hd=hd, scale=scale),
+        out_shape=(flat, flat, flat, flat, high, flat, high),
+        grid=(seq // bm,),
+        in_specs=[pl.BlockSpec((bm, dim), lambda i: (i, 0)), pl.BlockSpec((dim, 3 * hd), lambda i: (0, 0)), table, table, gain, gain],
+        out_specs=(tile, tile, tile, tile, tall, tile, tall),
+        compiler_params=pltpu.CompilerParams(dimension_semantics=('arbitrary',), vmem_limit_bytes=40 * 1024 * 1024),
+        cost_estimate=pl.CostEstimate(flops=6 * seq * dim * hd, bytes_accessed=seq * dim * 2 + seq * hd * 18, transcendentals=0),
+        name='qkv',
+    )(h, w, cos_t, sin_t, qg, kg)
+
+
+def norm_back(x_raw, dy, gain):
+    x = x_raw.astype(F32)
+    r = lax.rsqrt(jnp.mean(x * x, axis=-1, keepdims=True) + EPS)
+    xr = x * r
+    g_gain = jnp.sum(dy * xr, axis=0, keepdims=True)
+    dx = dy * (1.0 + gain)
+    return r * (dx - xr * jnp.mean(dx * xr, axis=-1, keepdims=True)), g_gain
+
+
+def head_back_body(even_ref, dq_ref, keep_ref, got_ref, qr_ref, kr_ref, cos_ref, sin_ref, qg_ref, kg_ref, out_ref, gq_ref, gk_ref, *, hd):
+    @pl.when(pl.program_id(0) == 0)
+    def _():
+        gq_ref[...] = jnp.zeros_like(gq_ref)
+        gk_ref[...] = jnp.zeros_like(gk_ref)
+
+    cos_t, sin_t = cos_ref[...], sin_ref[...]
+    dq, gq = norm_back(qr_ref[...], turn_back(dq_ref[...].astype(F32), cos_t, sin_t), qg_ref[...])
+    out_ref[:, :hd] = dq.astype(BF)
+    gq_ref[...] += gq
+    d_kv = (keep_ref[...] + got_ref[...]).astype(BF)
+
+    @pl.when(even_ref[0] == 1)
+    def _():
+        dk, gk = norm_back(kr_ref[...], turn_back(d_kv.astype(F32), cos_t, sin_t), kg_ref[...])
+        out_ref[:, hd:] = dk.astype(BF)
+        gk_ref[...] += gk
+
+    @pl.when(even_ref[0] == 0)
+    def _():
+        out_ref[:, hd:] = d_kv
+
+
+def head_back(even, dq, keep, got, qr, kr, cos_t, sin_t, qg, kg, bm):
+    seq, hd = dq.shape
+    tile = pl.BlockSpec((bm, hd), lambda i, s: (i, 0))
+    table = pl.BlockSpec((bm, hd // 2), lambda i, s: (i, 0))
+    gain = pl.BlockSpec((1, hd), lambda i, s: (0, 0))
+    vec = jax.ShapeDtypeStruct((1, hd), F32)
+    return pl.pallas_call(
+        functools.partial(head_back_body, hd=hd),
+        out_shape=(jax.ShapeDtypeStruct((seq, 2 * hd), BF), vec, vec),
+        grid_spec=pltpu.PrefetchScalarGridSpec(
+            num_scalar_prefetch=1,
+            grid=(seq // bm,),
+            in_specs=[tile, tile, tile, tile, tile, table, table, gain, gain],
+            out_specs=(pl.BlockSpec((bm, 2 * hd), lambda i, s: (i, 0)), gain, gain),
+        ),
+        compiler_params=pltpu.CompilerParams(dimension_semantics=('arbitrary',), vmem_limit_bytes=40 * 1024 * 1024),
+        cost_estimate=pl.CostEstimate(flops=40 * seq * hd * 100, bytes_accessed=seq * hd * 22, transcendentals=0),
+        name='head_back',
+    )(even, dq, keep, got, qr, kr, cos_t, sin_t, qg, kg)
 
 
 def solution(mesh):
@@ -223,26 +326,24 @@
 
         pooled_rows = mm(sel, pooled_all).astype(BF)
         normed_rows, norm_pull = jax.vjp(gain_norm, pooled_rows, pn_f)
+        flat_all = jnp.where(jnp.any(in_all, axis=1), jnp.sum(jnp.where(in_all, jnp.arange(n_img)[None, :] * block + off_all, 0), axis=1), -1)
+        sel_all = (flat_all[:, None] == jnp.arange(n_img * block)[None, :]).astype(BF)
+        normed_pos = mm(sel_all, gain_norm(pooled_all, pn_f)).astype(BF)
         soft_rows = mm(normed_rows, w_proj).astype(BF)
         merged = jnp.where(img_mask, soft_rows, text_loc)
         hidden, pre_pull = jax.vjp(gain_norm, merged, pre_f)
         hidden_all = lax.all_gather(hidden, 'cp', tiled=True)
 
+        cos_t, sin_t = rope_tables(pos_all, hd)
         kv_id = rank * kv_heads // size
         wq_h = lax.dynamic_slice(w_query, (0, rank * hd), (dim, hd))
         wk_h = lax.dynamic_slice(w_key, (0, kv_id * hd), (dim, hd))
         wv_h = lax.dynamic_slice(w_value, (0, kv_id * hd), (dim, hd))
         wo_h = lax.dynamic_slice(w_out, (rank * hd, 0), (hd, dim))
-        q_raw = mm(hidden_all, wq_h).astype(BF)
-        k_raw = mm(hidden_all, wk_h).astype(BF)
-        v = mm(hidden_all, wv_h).astype(BF)
-        cos_t, sin_t = rope_tables(pos_all, hd)
-        rot = functools.partial(head_rotate, cos_t=cos_t, sin_t=sin_t)
-        q, q_pull = jax.vjp(rot, q_raw, qg_f)
-        k, k_pull = jax.vjp(rot, k_raw, kg_f)
-        qs = (q.astype(F32) * scale).astype(BF)
-
-        o, o_wide, lse = attn_fwd(qs, k, v.T, lim, lmax, bq, block)
+        w_head = jnp.concatenate([wq_h, wk_h, wv_h], axis=1)
+        q_raw, k_raw, qs, k, kt, v, vt = qkv_call(hidden_all, w_head, cos_t, sin_t, qg_f[None], kg_f[None], bq, scale)
+
+        o, o_wide, lse = attn_fwd(qs, k, vt, lim, lmax, bq, block)
         o_rows = lax.all_to_all(o.reshape(size, loc, hd), 'cp', 0, 0, tiled=True)
         o_rows = o_rows.transpose(1, 0, 2).reshape(loc, heads * hd)
         proj_out = mm(o_rows, w_out).astype(BF)
@@ -252,18 +353,17 @@
         d_proj_all = lax.all_gather(d_proj, 'cp', tiled=True)
         d_o = mm(d_proj_all, wo_h, ((1,), (1,))).astype(BF)
         g_out_h = mm(o, d_proj_all, ((0,), (0,))).astype(BF)
+        d_o, g_out_h = lax.optimization_barrier((d_o, g_out_h))
         g_out = lax.all_gather(g_out_h, 'cp', tiled=True)
         delta = jnp.sum(d_o.astype(F32) * o_wide, axis=1).reshape(nq, 1, bq)
-        d_q, d_k_part, d_v_part = attn_bwd(qs, k, k.T, v, d_o, lse, delta, lim, lmax, bq, block, scale)
-        swap = [(i, i ^ 1) for i in range(size)]
-        got = lax.ppermute(jnp.where(even, d_v_part, d_k_part), 'cp', swap)
-        d_kv = (jnp.where(even, d_k_part, d_v_part) + got).astype(BF)
-        d_q_raw, g_q_gain = q_pull(d_q)
-        d_k_raw, g_k_gain = k_pull(d_kv)
-        g_k_gain = jnp.where(even, g_k_gain, 0.0)
-        d_head = jnp.concatenate([d_q_raw, jnp.where(even, d_k_raw, d_kv)], axis=1)
+        flag = even.astype(jnp.int32).reshape(1)
+        d_q, keep, send = attn_bwd(qs, k, kt, v, d_o, lse, delta, lim, lmax, flag, bq, block, scale)
+        got = lax.ppermute(send, 'cp', [(i, i ^ 1) for i in range(size)])
+        d_head, g_q_gain, g_k_gain = head_back(flag, d_q, keep, got, q_raw, k_raw, cos_t, sin_t, qg_f[None], kg_f[None], bq)
+        g_q_gain, g_k_gain = g_q_gain[0], g_k_gain[0]
         d_rows = lax.all_to_all(d_head.reshape(size, loc, 2 * hd), 'cp', 0, 0, tiled=True)
         g_head = mm(hidden_all, d_head, ((0,), (0,))).astype(BF)
+        d_rows, g_head = lax.optimization_barrier((d_rows, g_head))
         g_head_all = lax.all_gather(g_head, 'cp')
         g_query = g_head_all[:, :, :hd].transpose(1, 0, 2).reshape(dim, heads * hd)
         g_key = g_head_all[0::2, :, hd:].transpose(1, 0, 2).reshape(dim, kv_heads * hd)
@@ -286,9 +386,10 @@
         spread = (d_pooled.astype(F32) / (POOL * POOL)).astype(BF)
         grad_vis = mm(pool_mat, spread, ((0,), (0,))).astype(BF)[None]
 
-        g_proj_part = mm(normed_rows, d_soft, ((0,), (0,)))
-        g_proj_loc = lax.psum_scatter(g_proj_part, 'cp', scatter_dimension=0, tiled=True).astype(BF)
-        g_proj = lax.all_gather(g_proj_loc, 'cp', tiled=True)
+        cols = dim // size
+        d_soft_cols = lax.all_to_all(d_soft.reshape(loc, size, cols).transpose(1, 0, 2), 'cp', 0, 0, tiled=True).reshape(seq, cols)
+        g_proj_loc = mm(d_soft_cols, normed_pos, ((0,), (0,))).astype(BF)
+        g_proj = lax.all_gather(g_proj_loc, 'cp', tiled=True).T
         small = lax.psum(jnp.concatenate([g_pn, g_pre, g_q_gain, g_k_gain, g_post]), 'cp').astype(BF)
         edges = [0, dim_v, dim_v + dim, dim_v + dim + hd, dim_v + dim + 2 * hd, dim_v + 2 * dim + 2 * hd]
         s_pn, s_pre, s_q, s_k, s_post = (small[a:b] for a, b in zip(edges[:-1], edges[1:]))

time: 944 us -> 814 us (0.86)
  other arithmetic: 116 us -> 32.9 us
  blocking collectives: 75.8 us -> 22.4 us
  Pallas kernels: 83 us -> 117 us
  waiting for transfers between devices: 409 us -> 384 us
  starting transfers between devices: 5.46 us -> 16.6 us
    all_to_all x0 -> x2, waiting for transfers between devices: none -> 70.6 us  [the longest x1 38.4 us: device_body(): lax.all_to_all(d_soft.reshape(loc, size, cols).transpose(1, 0, 2), 'cp',...]
    all_to_all x1 -> x0, blocking collectives: 52.9 us -> none  [device_body(): lax.all_to_all(d_head.reshape(size, loc, 2 * hd), 'cp', 0, 0, tiled=True)]
    reduce_sum x3 -> x1, other arithmetic: 41.4 us -> 2.28 us  [rms_scale(): return wide_vals * lax.rsqrt(mean_sq + EPS) * (1.0 + gain_vec)]
    reduce_scatter x1, waiting for transfers between devices: 34.7 us -> 0.01 us  [device_body(): lax.psum_scatter(d_pooled_all, 'cp', scatter_dimension=0, tiled=True)]
    pallas_call x0 -> x2, Pallas kernels: none -> 31.5 us  [the longest x1 22.8 us: qkv_call(): pl.pallas_call(functools.partial(qkv_body, hd=hd, scale=scale), out_shape...]
    all_gather x1, waiting for transfers between devices: 25.6 us -> 0.01 us  [device_body(): g_out = lax.all_gather(g_out_h, 'cp', tiled=True)]
    convert_element_type x2 -> x0, other arithmetic: 23 us -> none  [the longest x1 20.7 us: head_rotate(): return apply_rope(rms_scale(raw, gain), cos_t, sin_t).astype(BF)]
    reduce_scatter x1 -> x0, waiting for transfers between devices: 18.7 us -> none  [device_body(): lax.psum_scatter(g_proj_part, 'cp', scatter_dimension=0, tiled=True)]
  transfers between devices with their start and end apart: 10 -> 11, of which waited for: 9 -> 8; matrix products, arithmetic and copies ran while one was open for 11% -> 17% of each run, Pallas kernels for 0% -> 7%
where the time goes in v2:
time: 814 us; the launch traced here: 810 us
  waiting for transfers between devices  384 us (47%)
  matrix products  138 us (17%)
  Pallas kernels  117 us (14%)
  local copies, waits for them, and re-layouts  84.2 us (10%)
  other arithmetic  32.9 us (4%)
  blocking collectives  22.4 us (3%)
  starting transfers between devices  16.6 us (2%)
  between operations  15.1 us (2%)
    dot_general x14, matrix products, mm(): return lax.dot_general(a, b, (dims, ((), ())), preferred_element_type=F32)  138 us
    all_gather x1, waiting for transfers between devices, device_body(): d_proj_all = lax.all_gather(d_proj, 'cp', tiled=True)  89.7 us
    all_gather x1, waiting for transfers between devices, device_body(): g_head_all = lax.all_gather(g_head, 'cp')  82.3 us
    all_gather x1, waiting for transfers between devices, device_body(): hidden_all = lax.all_gather(hidden, 'cp', tiled=True)  74.7 us
    pallas_call x1, Pallas kernels, attn_bwd(): pl.pallas_call(body, out_shape=(jax.ShapeDtypeStruct((seq, hd), BF), jax....  47.7 us
    unnamed x104, local copies, waits for them, and re-layouts  45.9 us
    all_to_all x1, waiting for transfers between devices, device_body(): lax.all_to_all(d_soft.reshape(loc, size, cols).transpose(1, 0, 2), 'cp',...  38.4 us
    pallas_call x1, Pallas kernels, attn_fwd(): pl.pallas_call(body, out_shape=(jax.ShapeDtypeStruct((seq, hd), BF), jax....  37.6 us
  transfers between devices with their start and end apart: 11, of which 8 were waited for; matrix products, arithmetic and copies ran while one was open for 17% of the time, Pallas kernels for 7%

profile of v2, /device:TPU:113, one launch (start us, length us, event | category | flops | bytes accessed | tf_op | source)
XLA Modules:
  0.0 809.6 jit_solution(7422222467576506617)
XLA Ops:
  7.9 7.5 fusion.43
  16.4 32.4 %all-gather.8.cloned.1.call-done = bf16[2048,1152]{1,0:T(8,128)(2,1)} async-done(((bf16[256,1152]{1,0:T(8,128)(2,1)}), bf16[2048,1152]{1,0:T(8,128)(2,1)}) %all-gather.8.cloned.1.call-update) | async-done | bytes 4718608 | tf_op jit(solution)/shard_map/all_gather | solution.py:310
  54.3 6.8 fusion.21
  70.9 9.3 %multiply_sine_fusion = (f32[4096,128]{1,0:T(8,128)}, f32[4096,128]{1,0:T(8,128)}) fusion(f32[128]{0:T(128)S(1)} %multiply_power_fusion, f32[4096]{0:T(1024)S(1)} %convert_multiply_fusion.18), kind=kLoop, calls=%fused_computation.70 | loop fusion | flops 524288 | bytes 4211200 | tf_op jit(solution)/shard_map/sin | solution.py:32
  80.2 74.7 %all-gather.10.cloned.1.call-done.h_ref = bf16[4096,2304]{1,0:T(8,128)(2,1)} async-done(((bf16[512,2304]{1,0:T(8,128)(2,1)}), bf16[4096,2304]{1,0:T(8,128)(2,1)}) %all-gather.10.cloned.1.call-update) | async-done | bytes 18874384 | tf_op jit(solution)/shard_map/all_gather | solution.py:335
  154.9 22.8 %qkv.1 = (bf16[4096,256]{1,0:T(8,128)(2,1)S(1)}, bf16[4096,256]{1,0:T(8,128)(2,1)S(1)}, bf16[4096,256]{1,0:T(8,128)(2,1)S(1)}, bf16[4096,256]{1,0:T(8,128)(2,1)S...) custom-call(bf16[4096,2304]{1,0:T(8,128)(2,1)} %all-gather.10.cloned.1.call-done.h_ref,, ...), custom_call_target="tpu_custom_call" | custom-call | flops 14495514624 | bytes 37748736 | tf_op jit(solution)/shard_map/qkv/pallas_call | solution.py:218
  183.0 37.6 %attn_fwd.1 = (bf16[4096,256]{1,0:T(8,128)(2,1)S(1)}, f32[4096,256]{1,0:T(8,128)}, f32[8,1,512]{2,1,0:T(1,128)S(1)}) custom-call(s32[8]{0:T(128)S(1)} %select_reduce_fusion.2.lmax_ref, s32[8,1,512]{2,1,0:T(1,128)S(1)} %add_select_fusion.2.lim_ref, bf16[4096,256]{1,0:T(8,128)(2,1)S(1)} %get-tuple-element.33.q_ref, bf16[4096,256]{1,0:T(8,128)(2,1)} %copy-done.10, ...), custom_call_target="tpu_custom_call" | custom-call | flops 8589934592 | bytes 14680064 | tf_op jit(solution)/shard_map/attn_fwd/pallas_call | solution.py:88
  228.3 26.0 %all-to-all-done = bf16[8,512,256]{1,2,0:T(8,128)(2,1)} async-done(((bf16[8,512,256]{1,2,0:T(8,128)(2,1)}), bf16[8,512,256]{1,2,0:T(8,128)(2,1)}, u32[]{:S(2)}, u32[]{:S(2)}) %all-to-all-start) | async-done | bytes 2097184 | tf_op jit(solution)/shard_map/all_to_all | solution.py:347
  254.2 9.6 %fusion.19 = (f32[512]{0:T(512)S(1)}, bf16[512,2304]{1,0:T(8,128)(2,1)S(1)}) fusion(bf16[512,2048]{0,1:T(8,128)(2,1)} %bitcast.6, bf16[2048,2304]{1,0:T(8,128)(2,1)} %param.26), kind=kOutput, calls=%fused_computation.44 | convolution fusion | flops 4836556288 | bytes 13895680 | tf_op jit(solution)/shard_map/dot_general | solution.py:40
  270.2 89.7 %all-gather.12.cloned.1.call-done = bf16[4096,2304]{1,0:T(8,128)(2,1)} async-done(((bf16[512,2304]{1,0:T(8,128)(2,1)}), bf16[4096,2304]{1,0:T(8,128)(2,1)}) %all-gather.12.cloned.1.call-update) | async-done | bytes 18874384 | tf_op jit(solution)/shard_map/all_gather | solution.py:353
  359.9 10.2 %convolution_convert_fusion.6 = bf16[256,2304]{1,0:T(8,128)(2,1)} fusion(bf16[4096,256]{1,0:T(8,128)(2,1)S(1)} %get-tuple-element.36, bf16[4096,2304]{1,0:T(8,128)(2,1)} %all-gather.12.cloned.1.call-done), kind=kOutput, calls=%fused_computation.66 | convolution fusion | flops 4832428032 | bytes 22151168 | tf_op jit(solution)/shard_map/dot_general | solution.py:40
  370.1 9.4 %convolution_convert_fusion.2.do_ref = bf16[4096,256]{1,0:T(8,128)(2,1)S(1)} fusion(bf16[4096,2304]{1,0:T(8,128)(2,1)} %all-gather.12.cloned.1.call-done, bf16[2048,2304]{1,0:T(8,128)(2,1)} %param.26, s32[]{:T(128)S(6)} %select_n.113), kind=kOutput, calls=%fused_computation.35 | convolution fusion | flops 4832886784 | bytes 22151172 | tf_op jit(solution)/shard_map/dot_general | solution.py:40
  383.7 47.7 %attn_bwd.1 = (bf16[4096,256]{1,0:T(8,128)(2,1)}, f32[4096,256]{1,0:T(8,128)}, f32[4096,256]{1,0:T(8,128)}) custom-call(s32[8]{0:T(128)} %copy-done.8, s32[1]{0:T(128)} %bitcast.7.even_ref, s32[8,1,512]{2,1,0:T(1,128)} %copy-done.7, f32[8,1,512]{2,1,0:T(1,128)} %copy-done.13, f32[8,1,512]{2,1,0:T(1,128)} %bitcast.90, bf16[4096,256]{1,0:T(8,128)(2,1)} %copy-done.9, ...), custom_call_target="tpu_custom_call" | custom-call | flops 21474836480 | bytes 20971520 | tf_op jit(solution)/shard_map/attn_bwd/pallas_call | solution.py:164
  431.7 7.0 collective-permute-done.got_ref
  443.9 8.7 %head_back.1 = (bf16[4096,512]{1,0:T(8,128)(2,1)}, f32[1,256]{1,0:T(1,128)S(1)}, f32[1,256]{1,0:T(1,128)S(1)}) custom-call(s32[1]{0:T(128)} %bitcast.7.even_ref, bf16[4096,256]{1,0:T(8,128)(2,1)S(1)} %copy-done.6, f32[4096,256]{1,0:T(8,128)} %get-tuple-element.43.keep_ref, f32[4096,256]{1,0:T(8,128)} %copy-done.21, bf16[4096,256]{1,0:T(8,128)(2,1)S(1)} %copy-done.3, ...), custom_call_target="tpu_custom_call" | custom-call | flops 4194304000 | bytes 23068672 | tf_op jit(solution)/shard_map/head_back/pallas_call | solution.py:268
  452.6 6.4 copy.42
  465.4 16.1 %convolution_convert_fusion.5 = bf16[2304,512]{1,0:T(8,128)(2,1)} fusion(bf16[4096,2304]{1,0:T(8,128)(2,1)} %all-gather.10.cloned.1.call-done.h_ref, bf16[4096,512]{1,0:T(8,128)(2,1)} %get-tuple-element.47), kind=kOutput, calls=%fused_computation.56 | convolution fusion | flops 9664856064 | bytes 25427968 | tf_op jit(solution)/shard_map/dot_general | solution.py:40
  481.5 32.1 %all-to-all-done.1 = bf16[8,512,512]{1,2,0:T(8,128)(2,1)} async-done(((bf16[8,512,512]{1,2,0:T(8,128)(2,1)}), bf16[8,512,512]{1,2,0:T(8,128)(2,1)}, u32[]{:S(2)}, u32[]{:S(2)}) %all-to-all-start.1) | async-done | bytes 4194336 | tf_op jit(solution)/shard_map/all_to_all | solution.py:364
  517.1 6.8 fusion.96
  523.8 11.5 %convolution_add_fusion = f32[512,2304]{1,0:T(8,128)} fusion(f32[512,2304]{1,0:T(8,128)} %fusion.96, bf16[512,2048]{0,1:T(8,128)(2,1)S(1)} %bitcast.84, bf16[2304,2048]{1,0:T(8,128)(2,1)} %param.21), kind=kOutput, calls=%fused_computation.36 | convolution fusion | flops 4833017856 | bytes 20971520 | tf_op jit(solution)/shard_map/dot_general | solution.py:40
  535.3 6.0 fusion.14
  544.6 6.0 fusion.47
  566.3 38.4 %all-to-all-done.2 = bf16[8,512,288]{1,2,0:T(8,128)(2,1)S(1)} async-done(((bf16[8,512,288]{1,2,0:T(8,128)(2,1)}), bf16[8,512,288]{1,2,0:T(8,128)(2,1)S(1)}, u32[]{:S(2)}, u32[]{:S(2)}) %all-to-all-start.2) | async-done | bytes 2359328 | tf_op jit(solution)/shard_map/all_to_all | solution.py:390
  606.5 30.5 %fusion.40 = bf16[288,1152]{1,0:T(8,128)(2,1)} fusion(bf16[4096,288]{0,1:T(8,128)(2,1)} %bitcast.83, s32[4096]{0:T(1024)S(1)} %broadcast_select_fusion.2, bf16[2048,1152]{1,0:T(8,128)(2,1)} %all-gather.8.cloned.1.call-done, f32[1152]{0:T(1024)S(1)} %copy-done.33, f32[2048]{0:T(1024)S(1)} %add_rsqrt_fusion), kind=kOutput, calls=%fused_computation.78 | convolution fusion | flops 22068137984 | bytes 7770624 | tf_op jit(solution)/shard_map/dot_general | solution.py:40
  638.0 22.4 %psum.7 = bf16[6272]{0:T(1024)(128)(2,1)S(1)} all-reduce(f32[6272]{0:T(1024)S(1)} %constant_dynamic-update-slice_fusion), channel_id=1, replica_groups=mesh['dp'=2,'cp'=8] {'cp'}, use_global_device_ids=true, to_apply=%region_16.17 | all-reduce | flops 6272 | bytes 37632 | tf_op jit(solution)/shard_map/psum | solution.py:393
  663.7 6.9 fusion.3
  670.6 8.5 %copy.48 = bf16[1152,2304]{1,0:T(8,128)(2,1)} copy(bf16[1152,2304]{0,1:T(8,128)(2,1)} %bitcast.79) | data formatting | bytes 10616832
  679.2 82.3 %all-gather.18.cloned.1.call-done = bf16[18432,512]{1,0:T(8,128)(2,1)} async-done(((bf16[2304,512]{1,0:T(8,128)(2,1)}), bf16[18432,512]{1,0:T(8,128)(2,1)}) %all-gather.18.cloned.1.call-update) | async-done | bytes 18874384 | tf_op jit(solution)/shard_map/all_gather | solution.py:367
  761.5 8.0 slice_bitcast_fusion
  769.5 8.1 slice_bitcast_fusion.1
  777.6 8.8 %copy.50 = bf16[8,288,8,256]{3,2,0,1:T(8,128)(2,1)} copy(bf16[8,288,8,256]{3,2,1,0:T(8,128)(2,1)} %slice_bitcast_fusion) | data formatting | bytes 18874368 | tf_op jit(solution)/shard_map/reshape | solution.py:368
  794.5 8.0 copy.59
  (174 shorter events, 88.4 us)
Async XLA Ops:
  7.2 41.6 %all-gather.8.cloned.1.call-start = ((), (), s32[]{:S(2)}) async-start(), calls=%async_computation.4 | async-start | bytes 5308416 | tf_op jit(solution)/shard_map/all_gather | solution.py:310
  7.9 8.2 %copy-start.29 = (s32[8]{0:T(128)S(1)}, s32[8]{0:T(128)}, u32[]{:S(2)}) copy-start(s32[8]{0:T(128)} %param.16) | copy-start | bytes 100
  7.9 8.4 %copy-start.36 = (bf16[1152]{0:T(1024)(128)(2,1)S(1)}, bf16[1152]{0:T(1024)(128)(2,1)}, u32[]{:S(2)}) copy-start(bf16[1152]{0:T(1024)(128)(2,1)} %param.18) | copy-start | bytes 6916
  7.9 8.4 %copy-start.34 = (bf16[2304]{0:T(1024)(128)(2,1)S(1)}, bf16[2304]{0:T(1024)(128)(2,1)}, u32[]{:S(2)}) copy-start(bf16[2304]{0:T(1024)(128)(2,1)} %param.20) | copy-start | bytes 13828
  15.5 139.4 %all-gather.10.cloned.1.call-start = ((), (), s32[]{:S(2)}) async-start(), calls=%async_computation.5 | async-start | bytes 21233664 | tf_op jit(solution)/shard_map/all_gather | solution.py:335
  16.3 37.9 %copy-start.37 = (s32[512]{0:T(512)}, s32[512]{0:T(512)S(1)}, u32[]{:S(2)}) copy-start(s32[512]{0:T(512)S(1)} %broadcast_select_fusion.3) | copy-start | bytes 6148
  16.3 37.9 %copy-start.32 = (f32[1152]{0:T(1024)}, f32[1152]{0:T(1024)S(1)}, u32[]{:S(2)}) copy-start(f32[1152]{0:T(1024)S(1)} %convert_add_fusion.4) | copy-start | bytes 13828
  16.4 37.9 %copy-start.41 = (bf16[512,2304]{1,0:T(8,128)(2,1)S(1)}, bf16[512,2304]{1,0:T(8,128)(2,1)}, u32[]{:S(2)}) copy-start(bf16[512,2304]{1,0:T(8,128)(2,1)} %param.15) | copy-start | bytes 7077892
  65.8 117.2 %copy-start.8 = (s32[8]{0:T(128)}, s32[8]{0:T(128)S(1)}, u32[]{:S(2)}) copy-start(s32[8]{0:T(128)S(1)} %select_reduce_fusion.2.lmax_ref) | copy-start | bytes 100
  65.8 117.2 %copy-start.7 = (s32[8,1,512]{2,1,0:T(1,128)}, s32[8,1,512]{2,1,0:T(1,128)S(1)}, u32[]{:S(2)}) copy-start(s32[8,1,512]{2,1,0:T(1,128)S(1)} %add_select_fusion.2.lim_ref) | copy-start | bytes 49156
  183.0 37.6 %copy-start.9 = (bf16[4096,256]{1,0:T(8,128)(2,1)}, bf16[4096,256]{1,0:T(8,128)(2,1)S(1)}, u32[]{:S(2)}) copy-start(bf16[4096,256]{1,0:T(8,128)(2,1)S(1)} %get-tuple-element.33.q_ref) | copy-start | bytes 6291460
  183.0 37.6 %copy-start.12 = (bf16[4096,256]{1,0:T(8,128)(2,1)}, bf16[4096,256]{1,0:T(8,128)(2,1)S(1)}, u32[]{:S(2)}) copy-start(bf16[4096,256]{1,0:T(8,128)(2,1)S(1)} %get-tuple-element.41.v_ref) | copy-start | bytes 6291460
  223.6 30.7 %all-to-all-start = ((bf16[8,512,256]{1,2,0:T(8,128)(2,1)}), bf16[8,512,256]{1,2,0:T(8,128)(2,1)}, u32[]{:S(2)}, u32[]{:S(2)}) async-start(bf16[8,512,256]{1,2,0:T(8,128)(2,1)} %copy.41), calls=%async_computation | async-start | bytes 4194304 | tf_op jit(solution)/shard_map/all_to_all | solution.py:347
  228.0 131.9 %all-gather.12.cloned.1.call-start = ((), (), s32[]{:S(2)}) async-start(), calls=%async_computation.6 | async-start | bytes 21233664 | tf_op jit(solution)/shard_map/all_gather | solution.py:353
  254.2 9.6 %copy-start.17 = (bf16[512,2304]{1,0:T(8,128)(2,1)S(1)}, bf16[512,2304]{1,0:T(8,128)(2,1)}, u32[]{:S(2)}) copy-start(bf16[512,2304]{1,0:T(8,128)(2,1)} %param.17) | copy-start | bytes 7077892
  270.2 393.6 %all-gather.16.cloned.1.call-start = ((), (), s32[]{:S(2)}) async-start(), calls=%async_computation.9 | async-start | bytes 10616832 | tf_op jit(solution)/shard_map/all_gather | solution.py:357
  383.7 56.9 %copy-start = (f32[4096,128]{1,0:T(8,128)S(1)}, f32[4096,128]{1,0:T(8,128)}, u32[]{:S(2)}) copy-start(f32[4096,128]{1,0:T(8,128)} %get-tuple-element.108.sin_ref) | copy-start | bytes 6291460
  383.7 57.0 %copy-start.1 = (f32[4096,128]{1,0:T(8,128)S(1)}, f32[4096,128]{1,0:T(8,128)}, u32[]{:S(2)}) copy-start(f32[4096,128]{1,0:T(8,128)} %get-tuple-element.109.cos_ref) | copy-start | bytes 6291460
  383.7 57.0 %copy-start.3 = (bf16[4096,256]{1,0:T(8,128)(2,1)S(1)}, bf16[4096,256]{1,0:T(8,128)(2,1)}, u32[]{:S(2)}) copy-start(bf16[4096,256]{1,0:T(8,128)(2,1)} %copy-done.2) | copy-start | bytes 6291460
  431.4 7.2 collective-permute-start
  459.0 54.6 %all-to-all-start.1 = ((bf16[8,512,512]{1,2,0:T(8,128)(2,1)}), bf16[8,512,512]{1,2,0:T(8,128)(2,1)}, u32[]{:S(2)}, u32[]{:S(2)}) async-start(bf16[8,512,512]{1,2,0:T(8,128)(2,1)} %copy.42), calls=%async_computation.1 | async-start | bytes 8388608 | tf_op jit(solution)/shard_map/all_to_all | solution.py:364
  465.0 198.8 %reduce-scatter.2.cloned.1.call-start = ((), (), s32[]{:S(2)}) async-start(), calls=%async_computation.7 | async-start | bytes 5308416 | tf_op jit(solution)/shard_map/reduce_scatter | solution.py:385
  517.0 18.2 %slice-start = ((s8[4718592]{0:T(1024)(128)(4,1)}), s8[524288]{0:T(1024)(128)(4,1)S(1)}, s32[]{:S(2)}) async-start(s8[4718592]{0:T(1024)(128)(4,1)} %bitcast.87), calls=%async_computation.11 | async-start | bytes 1048576
  523.8 11.5 %copy-start.16 = (bf16[512,2304]{1,0:T(8,128)(2,1)S(1)}, bf16[512,2304]{1,0:T(8,128)(2,1)}, u32[]{:S(2)}) copy-start(bf16[512,2304]{1,0:T(8,128)(2,1)} %copy-done.14) | copy-start | bytes 7077892
  523.8 11.5 %slice-start.1 = ((s8[4718592]{0:T(1024)(128)(4,1)}), s8[4194304]{0:T(1024)(128)(4,1)S(1)}, s32[]{:S(2)}) async-start(s8[4718592]{0:T(1024)(128)(4,1)} %bitcast.87), calls=%async_computation.12 | async-start | bytes 8388608
  555.9 7.1 copy-start.26
  558.3 46.4 %all-to-all-start.2 = ((bf16[8,512,288]{1,2,0:T(8,128)(2,1)}), bf16[8,512,288]{1,2,0:T(8,128)(2,1)S(1)}, u32[]{:S(2)}, u32[]{:S(2)}) async-start(bf16[8,512,288]{1,2,0:T(8,128)(2,1)} %bitcast.78), calls=%async_computation.3 | async-start | bytes 4718592 | tf_op jit(solution)/shard_map/all_to_all | solution.py:390
  562.9 107.7 %all-gather.14.cloned.1.call-start = ((), (), s32[]{:S(2)}) async-start(), calls=%async_computation.8 | async-start | bytes 5971968 | tf_op jit(solution)/shard_map/all_gather | solution.py:392
  606.5 31.5 %copy-start.28 = (f32[2304]{0:T(1024)S(1)}, f32[2304]{0:T(1024)}, u32[]{:S(2)}) copy-start(f32[2304]{0:T(1024)} %get-tuple-element.92) | copy-start | bytes 27652
  637.0 25.1 %copy-start.20 = (bf16[512,2304]{1,0:T(8,128)(2,1)S(1)}, bf16[512,2304]{1,0:T(8,128)(2,1)}, u32[]{:S(2)}) copy-start(bf16[512,2304]{1,0:T(8,128)(2,1)} %get-tuple-element.101) | copy-start | bytes 7077892
  637.0 26.7 %copy-start.24 = (s32[4096]{0:T(1024)S(1)}, s32[4096]{0:T(1024)}, u32[]{:S(2)}) copy-start(s32[4096]{0:T(1024)} %copy-done.23) | copy-start | bytes 49156
  637.1 124.4 %all-gather.18.cloned.1.call-start = ((), (), s32[]{:S(2)}) async-start(), calls=%async_computation.10 | async-start | bytes 21233664 | tf_op jit(solution)/shard_map/all_gather | solution.py:367
  (27 other events, 100.9 us)
Sparse Core Ops, SparseCore 0:
  15.6 33.1 all-gather.7
  64.8 90.0 all-gather.9
  270.3 89.5 all-gather.11
  379.7 50.4 all-gather.15
  556.0 54.9 reduce-scatter.1
  637.2 32.0 all-gather.13
  671.4 89.9 all-gather.17
